TPU v7x, 16 devices: a 4x2x1 block of a 4x4x8 slice. The times are simulated.
16 devices in a mesh: dp: 4 (over y, z, core), ep: 4 (over x).
Axes of the slice: x: 4, y: 2, z: 1, core: 2. Of those that a mesh axis runs over, the one named last changes fastest.
The devices are a block of a 4x4x8 slice.
Arguments:
- x: bfloat16 [4, 4, 768, 2048], P('dp', 'ep'), parts along dimension 0
- expert: int32 [4, 4, 768, 6], P('dp', 'ep'), parts along dimension 0
- slot: int32 [4, 4, 768, 6], P('dp', 'ep'), parts along dimension 0
- gate: float32 [4, 4, 768, 6], P('dp', 'ep'), parts along dimension 0
- w_gate: bfloat16 [64, 2048, 1408], P('ep')
- w_up: bfloat16 [64, 2048, 1408], P('ep')
- w_down: bfloat16 [64, 1408, 2048], P('ep')
- s_gate: bfloat16 [2048, 2816], replicated
- s_up: bfloat16 [2048, 2816], replicated
- s_down: bfloat16 [2816, 2048], replicated
Outputs:
- y: bfloat16 [4, 4, 768, 2048], P('dp', 'ep'), parts along dimension 0
There are 4 independent parts. A program takes and returns all parts, laid end to end along the dimension named above; an argument that names none is the same for every part.
All inputs are finite; a program needn't handle non-finite values.
Results may differ from a plain program's by a relative error of at most 0.009.
Values are sent between devices in bfloat16 or wider.
A program may use at most 768 MiB of HBM per device.

v0:
```python
import jax
import jax.numpy as jnp
from jax import lax
from jax.sharding import NamedSharding, PartitionSpec as P


def einsum(form, a, b):
    return jnp.einsum(form, a.astype(jnp.float32), b.astype(jnp.float32))


def for_all(x, s_gate, s_up, s_down):
    h = jax.nn.silu(einsum("...d,df->...f", x, s_gate)) * einsum("...d,df->...f", x, s_up)
    return einsum("...f,fd->...d", h.astype(jnp.bfloat16), s_down)


def solution(mesh):
    def placed(v, *spec):
        return lax.with_sharding_constraint(v, NamedSharding(mesh, P(*spec)))

    def step(x, expert, slot, gate, w_gate, w_up, w_down, s_gate, s_up, s_down):
        experts, (tokens, top) = w_gate.shape[0], expert.shape[2:]
        slots = 5 * tokens * top // (4 * experts)
        to_expert = jax.nn.one_hot(expert, experts, dtype=jnp.bfloat16)
        to_slot = jax.nn.one_hot(slot, slots, dtype=jnp.bfloat16)
        weighted = to_expert * gate[..., None].astype(jnp.bfloat16)
        dispatch = einsum("abtke,abtkc->abtec", to_expert, to_slot).astype(jnp.bfloat16)
        combine = einsum("abtke,abtkc->abtec", weighted, to_slot).astype(jnp.bfloat16)
        z = einsum("abtec,abtd->aebcd", dispatch, x).astype(jnp.bfloat16)
        z = placed(z, "dp", None, "ep", None, None)
        z = placed(z, "dp", "ep", None, None, None)
        h = jax.nn.silu(einsum("aebcd,edf->aebcf", z, w_gate))
        h = (h * einsum("aebcd,edf->aebcf", z, w_up)).astype(jnp.bfloat16)
        out = einsum("aebcf,efd->aebcd", h, w_down).astype(jnp.bfloat16)
        out = placed(out, "dp", "ep", None, None, None)
        out = placed(out, "dp", None, "ep", None, None)
        y = einsum("abtec,aebcd->abtd", combine, out)
        return (y + for_all(x, s_gate, s_up, s_down)).astype(jnp.bfloat16)

    return step
```

profile of v0, /device:TPU:112, one launch (start us, length us, event | category | flops | bytes accessed | tf_op | source)
XLA Modules:
  0.0 1076.4 jit_solution(15854442883618663174)
XLA Ops:
  0.0 0.0 copy-start
  0.0 1.0 copy.25
  1.1 0.0 copy-start.2
  1.1 1.7 copy.27
  2.7 11.9 %convolution_convert_fusion.1 = bf16[768,64,90]{2,1,0:T(8,128)(2,1)S(1)} fusion(s32[768,6]{1,0:T(8,128)} %bitcast.123, s32[768,6]{1,0:T(8,128)S(1)} %bitcast.121), kind=kOutput, calls=%fused_computation.28 | convolution fusion | flops 58217472 | bytes 8884224 | tf_op jit(solution)/abtke,abtkc->abtec/dot_general | solution.py:8
  14.7 0.0 copy-done
  14.7 47.5 %convolution_convert_fusion = bf16[64,90,2048]{2,1,0:T(8,128)(2,1)} fusion(bf16[768,64,90]{2,1,0:T(8,128)(2,1)S(1)} %convolution_convert_fusion.1, bf16[1,1,768,2048]{3,2,1,0:T(8,128)(2,1)S(1)} %copy-done), kind=kOutput, calls=%fused_computation.19 | convolution fusion | flops 18131189760 | bytes 35586048 | tf_op jit(solution)/abtec,abtd->aebcd/dot_general | solution.py:8
  62.2 0.0 copy-done.2
  62.2 22.2 %copy.14 = bf16[1,4,16,1,90,2048]{5,2,4,3,0,1:T(8,128)(2,1)S(1)} copy(bf16[1,4,16,1,90,2048]{5,4,2,1,3,0:T(8,128)(2,1)} %bitcast.119) | data formatting | bytes 47185920 | tf_op jit(solution)/sharding_constraint;jit(solution)/sharding_constraint | solution.py:18
  84.4 262.7 %all-to-all.4 = bf16[1,4,16,1,90,2048]{5,2,4,3,0,1:T(8,128)(2,1)} all-to-all(bf16[1,4,16,1,90,2048]{5,2,4,3,0,1:T(8,128)(2,1)S(1)} %copy.14), channel_id=1, replica_groups=mesh['dp'=4,'ep'=4] {'ep'}, dimensions={1} | all-to-all | bytes 47185920 | tf_op jit(solution)/sharding_constraint;jit(solution)/sharding_constraint | solution.py:18
  347.1 121.7 %fusion.2 = f32[16,4,90,1408]{3,2,1,0:T(8,128)} fusion(bf16[16,2048,1408]{2,1,0:T(8,128)(2,1)} %param.5, bf16[1,4,16,1,90,2048]{5,2,4,3,0,1:T(8,128)(2,1)} %all-to-all.4), kind=kOutput, calls=%fused_computation.2 | convolution fusion | flops 33218887680 | bytes 148307968 | tf_op jit(solution)/aebcd,edf->aebcf/dot_general | solution.py:8
  468.9 216.6 %fusion.6 = bf16[1,16,4,90,1408]{4,3,2,1,0:T(8,128)(2,1)} fusion(f32[16,4,90,1408]{3,2,1,0:T(8,128)} %fusion.2, bf16[16,2048,1408]{2,1,0:T(8,128)(2,1)} %param.4, bf16[1,4,16,1,90,2048]{5,2,4,3,0,1:T(8,128)(2,1)} %all-to-all.4), kind=kOutput, calls=%fused_computation.7 | convolution fusion | flops 33267548160 | bytes 164528128 | tf_op jit(solution)/aebcd,edf->aebcf/dot_general | solution.py:8
  685.5 53.8 %convert_bitcast_fusion = bf16[1,16,4,1,90,2048]{5,4,2,1,3,0:T(8,128)(2,1)} fusion(bf16[16,1408,2048]{2,1,0:T(8,128)(2,1)} %param.6, bf16[1,16,4,90,1408]{4,3,2,1,0:T(8,128)(2,1)} %fusion.6), kind=kOutput, calls=%fused_computation.15 | convolution fusion | flops 33230684160 | bytes 132087808 | tf_op jit(solution)/aebcf,efd->aebcd/dot_general | solution.py:8
  739.3 26.3 %copy.16 = bf16[1,16,4,1,90,2048]{5,1,4,3,0,2:T(8,128)(2,1)} copy(bf16[1,16,4,1,90,2048]{5,4,2,1,3,0:T(8,128)(2,1)} %convert_bitcast_fusion) | data formatting | bytes 47185920 | tf_op jit(solution)/sharding_constraint;jit(solution)/sharding_constraint | solution.py:18
  765.7 0.0 copy-start.3
  765.7 8.4 all-to-all-start.1
  774.1 1.3 convert_element_type.75
  775.4 1.6 copy.26
  777.0 0.0 copy-done.3
  777.0 14.3 %convolution_convert_fusion.2 = bf16[768,64,90]{2,1,0:T(8,128)(2,1)} fusion(s32[768,6]{1,0:T(8,128)} %bitcast.124, s32[768,6]{1,0:T(8,128)S(1)} %bitcast.122, bf16[768,6]{1,0:T(8,128)(2,1)} %bitcast.125), kind=kOutput, calls=%fused_computation.29 | convolution fusion | flops 58512384 | bytes 8893440 | tf_op jit(solution)/abtke,abtkc->abtec/dot_general | solution.py:8
  791.3 17.6 %copy.23 = bf16[768,64,90]{0,1,2:T(8,128)(2,1)} copy(bf16[768,64,90]{2,1,0:T(8,128)(2,1)} %convolution_convert_fusion.2) | data formatting | bytes 17694720 | tf_op jit(solution)/convert_element_type | solution.py:27
  809.0 15.0 %fusion.31 = f32[768,2816]{1,0:T(8,128)} fusion(bf16[2048,2816]{1,0:T(8,128)(2,1)} %param.7, bf16[1,1,768,2048]{3,2,1,0:T(8,128)(2,1)S(1)} %copy-done), kind=kOutput, calls=%fused_computation.36 | convolution fusion | flops 8858370048 | bytes 23330816 | tf_op jit(solution)/...d,df->...f/dot_general | solution.py:8
  824.0 31.0 %fusion.28 = f32[768,2048]{1,0:T(8,128)} fusion(bf16[2816,2048]{1,0:T(8,128)(2,1)} %param.9, bf16[2048,2816]{1,0:T(8,128)(2,1)} %param.8, f32[768,2816]{1,0:T(8,128)} %fusion.31, bf16[1,1,768,2048]{3,2,1,0:T(8,128)(2,1)S(1)} %copy-done), kind=kOutput, calls=%fused_computation.33 | convolution fusion | flops 17729716224 | bytes 41156608 | tf_op jit(solution)/...f,fd->...d/dot_general | solution.py:8
  855.0 175.3 %all-to-all-done.1 = bf16[1,16,4,1,90,2048]{5,1,4,3,0,2:T(8,128)(2,1)} async-done(((bf16[1,16,4,1,90,2048]{5,1,4,3,0,2:T(8,128)(2,1)}), bf16[1,16,4,1,90,2048]{5,1,4,3,0,2:T(8,128)(2,1)}, u32[]{:S(2)}, u32[]{:S(2)}) %all-to-all-start.1) | async-done | bytes 23592992 | tf_op jit(solution)/sharding_constraint;jit(solution)/sharding_constraint | solution.py:18
  1030.3 0.0 copy-start.1
  1030.3 0.0 copy-start.4
  1030.3 22.5 %copy.17 = bf16[1,16,4,1,90,2048]{5,1,2,4,3,0:T(8,128)(2,1)} copy(bf16[1,16,4,1,90,2048]{5,1,4,3,0,2:T(8,128)(2,1)} %all-to-all-done.1) | data formatting | bytes 47185920 | tf_op jit(solution)/sharding_constraint;jit(solution)/sharding_constraint | solution.py:18
  1052.7 0.0 copy-done.1
  1052.7 0.0 copy-done.4
  1052.8 23.2 %fusion.41 = bf16[1,1,768,2048]{3,2,1,0:T(8,128)(2,1)} fusion(f32[768,2048]{1,0:T(8,128)S(1)} %copy-done.4, bf16[768,64,90]{0,1,2:T(8,128)(2,1)S(1)} %copy-done.1, bf16[64,90,2048]{2,0,1:T(8,128)(2,1)} %bitcast.120), kind=kOutput, calls=%fused_computation.44 | convolution fusion | flops 18122539008 | bytes 41877504 | tf_op jit(solution)/abtec,aebcd->abtd/dot_general | solution.py:8
Async XLA Ops:
  0.0 14.7 %copy-start = (bf16[1,1,768,2048]{3,2,1,0:T(8,128)(2,1)S(1)}, bf16[1,1,768,2048]{3,2,1,0:T(8,128)(2,1)}, u32[]{:S(2)}) copy-start(bf16[1,1,768,2048]{3,2,1,0:T(8,128)(2,1)} %param.3) | copy-start | bytes 9437188
  1.1 61.1 %copy-start.2 = (s32[1,1,768,6]{3,2,1,0:T(8,128)}, s32[1,1,768,6]{3,2,1,0:T(8,128)S(1)}, u32[]{:S(2)}) copy-start(s32[1,1,768,6]{3,2,1,0:T(8,128)S(1)} %copy.25) | copy-start | bytes 55300
  765.7 11.3 %copy-start.3 = (s32[1,1,768,6]{3,2,1,0:T(8,128)S(1)}, s32[1,1,768,6]{3,2,1,0:T(8,128)}, u32[]{:S(2)}) copy-start(s32[1,1,768,6]{3,2,1,0:T(8,128)} %copy-done.2) | copy-start | bytes 55300
  765.7 264.6 %all-to-all-start.1 = ((bf16[1,16,4,1,90,2048]{5,1,4,3,0,2:T(8,128)(2,1)}), bf16[1,16,4,1,90,2048]{5,1,4,3,0,2:T(8,128)(2,1)}, u32[]{:S(2)}, u32[]{:S(2)}) async-start(bf16[1,16,4,1,90,2048]{5,1,4,3,0,2:T(8,128)(2,1)} %copy.16), calls=%async_computation.1 | async-start | bytes 47185920 | tf_op jit(solution)/sharding_constraint;jit(solution)/sharding_constraint | solution.py:18
  1030.3 22.5 %copy-start.1 = (bf16[768,64,90]{0,1,2:T(8,128)(2,1)S(1)}, bf16[768,64,90]{0,1,2:T(8,128)(2,1)}, u32[]{:S(2)}) copy-start(bf16[768,64,90]{0,1,2:T(8,128)(2,1)} %copy.23) | copy-start | bytes 26542084
  1030.3 22.5 %copy-start.4 = (f32[768,2048]{1,0:T(8,128)S(1)}, f32[768,2048]{1,0:T(8,128)}, u32[]{:S(2)}) copy-start(f32[768,2048]{1,0:T(8,128)} %fusion.28) | copy-start | bytes 18874372
where the time goes:
time: 1090 us; the launch traced here: 1080 us
  matrix products  535 us (49%)
  blocking collectives  263 us (24%)
  waiting for transfers between devices  175 us (16%)
  local copies, waits for them, and re-layouts  93 us (9%)
    dot_general x9, matrix products, einsum(): return jnp.einsum(form, a.astype(jnp.float32), b.astype(jnp.float32))  535 us
    another operation x1, blocking collectives, placed(): return lax.with_sharding_constraint(v, NamedSharding(mesh, P(*spec)))  263 us
    another operation x1, waiting for transfers between devices, placed(): return lax.with_sharding_constraint(v, NamedSharding(mesh, P(*spec)))  175 us
    another operation x3, local copies, waits for them, and re-layouts, placed(): return lax.with_sharding_constraint(v, NamedSharding(mesh, P(*spec)))  71 us
  transfers between devices with their start and end apart: 1, of which 1 were waited for; matrix products, arithmetic and copies ran while one was open for 8% of the time, Pallas kernels for 0%

commit v1 on v0

v1 whole, which is shorter than its diff:
```python
import functools

import jax
import jax.numpy as jnp
from jax import lax
from jax.experimental import pallas as pl
from jax.experimental.pallas import tpu as pltpu
from jax.sharding import PartitionSpec as P


CHUNKS = 4
UNIT = 16
BLOCK = 256
F32, BF16 = jnp.float32, jnp.bfloat16
VMEM_LIMIT = 60 * 1024 * 1024
ANY = pl.BlockSpec(memory_space=pl.ANY)
SMEM = pl.BlockSpec(memory_space=pltpu.SMEM)
VMEM = pl.BlockSpec(memory_space=pltpu.VMEM)


def params(**kw):
    return pltpu.CompilerParams(vmem_limit_bytes=VMEM_LIMIT, **kw)


def cost(flops, bytes_accessed):
    return pl.CostEstimate(flops=int(flops), bytes_accessed=int(bytes_accessed), transcendentals=0)


def column_tiles(width, tile):
    return [(c, min(tile, width - c)) for c in range(0, width, tile)]


def for_tiles(width, tile, body):
    whole = width // tile
    if whole:

        @pl.loop(0, whole)
        def _(i):
            body(pl.multiple_of(i * tile, tile), tile)

    if width % tile:
        body(whole * tile, width % tile)


def build_kernel(n_experts, meta, tab, onehot, comb, hits, weights, stage, hit_sem, comb_sem):
    s = pl.program_id(0)
    padded, tokens = tab.shape[1], hits.shape[1]
    ids = lax.broadcasted_iota(jnp.int32, (padded, tokens), 1).astype(F32)
    for e in range(n_experts):
        rows = pl.ds(pl.multiple_of(meta[4 + s, e] * UNIT, UNIT), padded)
        hit = tab[s, :, e : e + 1] == ids
        hits[rows, :] = jnp.where(hit, 1.0, 0.0).astype(BF16)
        weights[rows, :] = jnp.where(hit, tab[s, :, n_experts + e : n_experts + e + 1], 0.0).astype(BF16)

    total = meta[4 + s, n_experts - 1] + meta[s, n_experts - 1]
    per = BLOCK // UNIT
    blocks = (total + per - 1) // per

    @pl.loop(total, blocks * per)
    def _(u):
        rows = pl.ds(pl.multiple_of(u * UNIT, UNIT), UNIT)
        hits[rows, :] = jnp.zeros((UNIT, tokens), BF16)
        weights[rows, :] = jnp.zeros((UNIT, tokens), BF16)

    def block(b):
        return pl.ds(pl.multiple_of(b * BLOCK, BLOCK), BLOCK)

    def hit_copy(b):
        return pltpu.make_async_copy(hits.at[block(b)], onehot.at[s, b], hit_sem.at[b])

    def comb_copy(b):
        return pltpu.make_async_copy(stage.at[b], comb.at[s, b], comb_sem.at[b])

    @pl.loop(0, blocks)
    def _(b):
        hit_copy(b).start()
        stage[b] = weights[block(b), :].T
        comb_copy(b).start()

    @pl.loop(0, blocks)
    def _(b):
        hit_copy(b).wait()
        comb_copy(b).wait()


def build(meta, tab, tokens, slots_padded):
    n_experts = meta.shape[1]
    rows = n_experts * slots_padded
    blocks = rows // BLOCK
    return pl.pallas_call(
        functools.partial(build_kernel, n_experts),
        grid=(4,),
        out_shape=[
            jax.ShapeDtypeStruct((4, blocks, BLOCK, tokens), BF16),
            jax.ShapeDtypeStruct((4, blocks, tokens, BLOCK), BF16),
        ],
        in_specs=[SMEM, VMEM],
        out_specs=[ANY, ANY],
        scratch_shapes=[
            pltpu.VMEM((rows, tokens), BF16),
            pltpu.VMEM((rows, tokens), BF16),
            pltpu.VMEM((blocks, tokens, BLOCK), BF16),
            pltpu.SemaphoreType.DMA((blocks,)),
            pltpu.SemaphoreType.DMA((blocks,)),
        ],
        compiler_params=params(),
        cost_estimate=cost(1.5e10, 2e7),
        name="build",
    )(meta, tab)


def start_loads(pieces, x, x_sem):
    start, loads = 0, []
    for i, piece in enumerate(pieces):
        rows = piece.shape[0]
        copy = pltpu.make_async_copy(piece, x.at[pl.ds(start, rows)], x_sem.at[i])
        copy.start()
        loads.append(copy)
        start += rows
    return loads


def block_count(meta, s, n_experts):
    total = meta[4 + s, n_experts - 1] + meta[s, n_experts - 1]
    per = BLOCK // UNIT
    return (total + per - 1) // per


def dispatch_kernel(source, n_experts, meta, onehot, *refs):
    *pieces, z, x, hits, stage, x_sem, hit_sem, out_sem = refs
    width = x.shape[1]
    blocks = block_count(meta, source, n_experts)

    def hit_copy(b):
        return pltpu.make_async_copy(onehot.at[source, b], hits.at[b], hit_sem.at[b])

    def out_copy(b):
        rows = pl.ds(pl.multiple_of(b * BLOCK, BLOCK), BLOCK)
        return pltpu.make_async_copy(stage.at[b], z.at[rows], out_sem.at[b])

    loads = start_loads(pieces, x, x_sem)

    @pl.loop(0, blocks)
    def _(b):
        hit_copy(b).start()

    for copy in loads:
        copy.wait()

    @pl.loop(0, blocks)
    def _(b):
        hit_copy(b).wait()
        for c, n in column_tiles(width, 512):
            got = jnp.dot(hits[b], x[:, c : c + n], preferred_element_type=F32)
            stage[b, :, c : c + n] = got.astype(BF16)
        out_copy(b).start()

    @pl.loop(0, blocks)
    def _(b):
        out_copy(b).wait()


def dispatch(source, meta, onehot, pieces):
    n_experts = meta.shape[1]
    width = pieces[0].shape[1]
    _, blocks, _, tokens = onehot.shape
    return pl.pallas_call(
        functools.partial(dispatch_kernel, source, n_experts),
        out_shape=jax.ShapeDtypeStruct((blocks * BLOCK, width), BF16),
        in_specs=[SMEM, ANY] + [ANY] * len(pieces),
        out_specs=ANY,
        scratch_shapes=[
            pltpu.VMEM((tokens, width), BF16),
            pltpu.VMEM((blocks, BLOCK, tokens), BF16),
            pltpu.VMEM((blocks, BLOCK, width), BF16),
            pltpu.SemaphoreType.DMA((len(pieces),)),
            pltpu.SemaphoreType.DMA((blocks,)),
            pltpu.SemaphoreType.DMA((blocks,)),
        ],
        compiler_params=params(),
        cost_estimate=cost(5e9, 8e6),
    )(meta, onehot, *pieces)


def sizes(limit):
    return [m for m in (128, 256) if m < limit] + [limit]


def for_rows(rows, limit, body):
    low = 0
    for m in sizes(limit):
        pl.when((rows > low) & (rows <= m))(functools.partial(body, m))
        low = m


def up_kernel(n_experts, meta, onehot, z0, z1, z2, x_a, x_b, wg, wu, h, *scratch):
    gbuf, ubuf, x, hits, z3, zin, hst, g_sem, u_sem, x_sem, hit_sem, z_sem, h_sem = scratch
    zs = (z0, z1, z2)
    e, n = pl.program_id(0), pl.num_programs(0)
    slot = lax.rem(e, 2)
    deep = gbuf.shape[0]
    width, ff = x.shape[1], hst.shape[1]

    def unit(i):
        return pl.ds(pl.multiple_of(i * UNIT, UNIT), UNIT)

    def weight_copies(e):
        i = lax.rem(e, deep)
        return (
            pltpu.make_async_copy(wg.at[e], gbuf.at[i], g_sem.at[i]),
            pltpu.make_async_copy(wu.at[e], ubuf.at[i], u_sem.at[i]),
        )

    def in_copy(s, base, slot, k):
        return pltpu.make_async_copy(zs[s].at[unit(base)], zin.at[slot, unit(k)], z_sem.at[slot, k])

    def load(e, slot):
        k = 0
        for s in range(3):
            count, base = meta[s, e], meta[4 + s, e]

            @pl.loop(0, count)
            def _(u, s=s, k=k, base=base):
                in_copy(s, base + u, slot, k + u).start()

            k = k + count

    @pl.when(e == 0)
    def _():
        loads = start_loads((x_a, x_b), x, x_sem)
        blocks = block_count(meta, 3, n_experts)

        def hit_copy(b):
            return pltpu.make_async_copy(onehot.at[3, b], hits.at[b], hit_sem.at[b])

        @pl.loop(0, blocks)
        def _(b):
            hit_copy(b).start()

        load(e, slot)
        for i in range(deep):
            for copy in weight_copies(i):
                copy.start(priority=1)
        for copy in loads:
            copy.wait()

        @pl.loop(0, blocks)
        def _(b):
            hit_copy(b).wait()
            rows = pl.ds(pl.multiple_of(b * BLOCK, BLOCK), BLOCK)
            for c, size in column_tiles(width, 512):
                got = jnp.dot(hits[b], x[:, c : c + size], preferred_element_type=F32)
                z3[rows, c : c + size] = got.astype(BF16)

    @pl.when(e + 1 < n)
    def _():
        load(e + 1, 1 - slot)

    total = meta[8, e]
    fourth = total - meta[3, e]

    @pl.loop(0, meta[3, e])
    def _(u):
        zin[slot, unit(fourth + u), :] = z3[unit(meta[7, e] + u), :]

    @pl.loop(0, fourth)
    def _(k):
        in_copy(0, 0, slot, k).wait()

    def out_copy(e, m):
        dst = pl.ds(pl.multiple_of(meta[9, e] * UNIT, UNIT), m)
        return pltpu.make_async_copy(hst.at[pl.ds(0, m)], h.at[dst], h_sem)

    @pl.when(e > 0)
    def _():
        for_rows(meta[8, e - 1] * UNIT, zin.shape[1], lambda m: out_copy(e - 1, m).wait())

    for copy in weight_copies(e):
        copy.wait()
    place = lax.rem(e, deep)

    def compute(m):
        for c, size in column_tiles(ff, 256):
            rows = zin[slot, pl.ds(0, m), :]
            g = jnp.dot(rows, gbuf[place, :, c : c + size], preferred_element_type=F32)
            u = jnp.dot(rows, ubuf[place, :, c : c + size], preferred_element_type=F32)
            hst[pl.ds(0, m), c : c + size] = (jax.nn.silu(g) * u).astype(BF16)
        out_copy(e, m).start()

    for_rows(total * UNIT, zin.shape[1], compute)

    @pl.when(e + deep < n)
    def _():
        for copy in weight_copies(e + deep):
            copy.start(priority=1)

    @pl.when(e + 1 == n)
    def _():
        for_rows(total * UNIT, zin.shape[1], lambda m: out_copy(e, m).wait())


def gate_up(meta, onehot, zs, x_far, w_gate, w_up, slots_padded):
    n_experts, width, ff = w_gate.shape
    most = 4 * slots_padded
    _, blocks, _, tokens = onehot.shape
    deep = min(3, n_experts)
    return pl.pallas_call(
        functools.partial(up_kernel, n_experts),
        grid=(n_experts,),
        out_shape=jax.ShapeDtypeStruct((n_experts * most, ff), BF16),
        in_specs=[SMEM] + [ANY] * 8,
        out_specs=ANY,
        scratch_shapes=[
            pltpu.VMEM((deep, width, ff), BF16),
            pltpu.VMEM((deep, width, ff), BF16),
            pltpu.VMEM((tokens, width), BF16),
            pltpu.VMEM((blocks, BLOCK, tokens), BF16),
            pltpu.VMEM((blocks * BLOCK, width), BF16),
            pltpu.VMEM((2, most, width), BF16),
            pltpu.VMEM((most, ff), BF16),
            pltpu.SemaphoreType.DMA((deep,)),
            pltpu.SemaphoreType.DMA((deep,)),
            pltpu.SemaphoreType.DMA((2,)),
            pltpu.SemaphoreType.DMA((blocks,)),
            pltpu.SemaphoreType.DMA((2, most // UNIT)),
            pltpu.SemaphoreType.DMA,
        ],
        compiler_params=params(dimension_semantics=("arbitrary",)),
        cost_estimate=cost(6e10, 2e8),
        name="gate_up",
    )(meta, onehot, *zs, *x_far, w_gate, w_up)


def down_kernel(n_experts, start, meta, comb, h, wd, own, left_sum, left_send, right_sum, right_send, far_a, far_b, *scratch):
    hin, wbuf, ost, obuf, cbuf, acc, h_sem, w_sem, c_sem = scratch
    e, n = pl.program_id(0), pl.num_programs(0)
    deep = hin.shape[0]
    slot = lax.rem(e, deep)
    most, cols = ost.shape
    tokens = acc.shape[0]
    half = tokens // 2
    per = BLOCK // UNIT

    def unit(i):
        return pl.ds(pl.multiple_of(i * UNIT, UNIT), UNIT)

    def total_units(s):
        return meta[4 + s, n_experts - 1] + meta[s, n_experts - 1]

    def comb_copy(s, b):
        lanes = pl.ds(pl.multiple_of(b * BLOCK, BLOCK), BLOCK)
        return pltpu.make_async_copy(comb.at[s, b], cbuf.at[s, :, lanes], c_sem.at[s, b])

    def in_copy(e, m):
        rows = pl.ds(pl.multiple_of(meta[9, e] * UNIT, UNIT), m)
        i = lax.rem(e, deep)
        return pltpu.make_async_copy(h.at[rows], hin.at[i, pl.ds(0, m)], h_sem.at[i])

    def weight_copy(e):
        i = lax.rem(e, deep)
        return pltpu.make_async_copy(wd.at[e, :, pl.ds(start, cols)], wbuf.at[i], w_sem.at[i])

    def load(e):
        for_rows(meta[8, e] * UNIT, most, lambda m: in_copy(e, m).start())
        weight_copy(e).start()

    @pl.when(e == 0)
    def _():
        for i in range(deep):
            load(jnp.int32(i))
        for s in range(4):

            @pl.loop(0, block_count(meta, s, n_experts))
            def _(b, s=s):
                comb_copy(s, b).start()

    weight_copy(e).wait()

    def compute(m):
        in_copy(e, m).wait()
        for c, size in column_tiles(cols, 256):
            got = jnp.dot(hin[slot, pl.ds(0, m), :], wbuf[slot, :, c : c + size], preferred_element_type=F32)
            ost[pl.ds(0, m), c : c + size] = got.astype(BF16)

    for_rows(meta[8, e] * UNIT, most, compute)

    @pl.when(e + deep < n)
    def _():
        load(e + deep)

    padded = most // 4
    k = 0
    for s in range(4):
        to = pl.ds(pl.multiple_of(meta[4 + s, e] * UNIT, UNIT), padded)
        obuf[s, to, :] = ost[pl.ds(pl.multiple_of(k * UNIT, UNIT), padded), :]
        k = k + meta[s, e]

    @pl.when(e + 1 == n)
    def _():
        @pl.loop(0, 4)
        def _(s):
            blocks = block_count(meta, s, n_experts)

            @pl.loop(total_units(s), blocks * per)
            def _(u):
                obuf[s, unit(u), :] = jnp.zeros((UNIT, cols), BF16)

            @pl.loop(0, blocks)
            def _(b):
                comb_copy(s, b).wait()

            @pl.when(blocks == 0)
            def _():
                acc[...] = jnp.zeros_like(acc)

            for count in range(1, comb.shape[1] + 1):

                @pl.when(blocks == count)
                def _(depth=count * BLOCK):
                    def tile(c, size):
                        acc[:, pl.ds(c, size)] = jnp.dot(
                            cbuf[s, :, :depth], obuf[s, :depth, pl.ds(c, size)], preferred_element_type=F32
                        )

                    for_tiles(cols, 256, tile)

            @pl.when(s == 0)
            def _():
                own[...] = acc[...]

            @pl.when(s == 1)
            def _():
                left_send[...] = acc[pl.ds(0, half), :].astype(BF16)
                left_sum[...] = acc[pl.ds(half, half), :]

            @pl.when(s == 2)
            def _():
                right_sum[...] = acc[pl.ds(0, half), :]
                right_send[...] = acc[pl.ds(half, half), :].astype(BF16)

            @pl.when(s == 3)
            def _():
                far_a[...] = acc[pl.ds(0, half), :].astype(BF16)
                far_b[...] = acc[pl.ds(half, half), :].astype(BF16)


def down_combine(meta, comb, h, w_down, slots_padded, start, cols):
    n_experts, ff, width = w_down.shape
    tokens = comb.shape[2]
    most, rows = 4 * slots_padded, n_experts * slots_padded
    half = tokens // 2
    shapes = ((tokens, F32), (half, F32), (half, BF16), (half, F32), (half, BF16), (half, BF16), (half, BF16))
    deep = min(6, n_experts)
    whole = lambda r: pl.BlockSpec((r, cols), lambda e: (0, 0))
    return pl.pallas_call(
        functools.partial(down_kernel, n_experts, start),
        grid=(n_experts,),
        out_shape=[jax.ShapeDtypeStruct((r, cols), t) for r, t in shapes],
        in_specs=[SMEM, ANY, ANY, ANY],
        out_specs=[whole(r) for r, _ in shapes],
        scratch_shapes=[
            pltpu.VMEM((deep, most, ff), BF16),
            pltpu.VMEM((deep, ff, cols), BF16),
            pltpu.VMEM((most, cols), BF16),
            pltpu.VMEM((4, rows, cols), BF16),
            pltpu.VMEM((4, tokens, rows), BF16),
            pltpu.VMEM((tokens, cols), F32),
            pltpu.SemaphoreType.DMA((deep,)),
            pltpu.SemaphoreType.DMA((deep,)),
            pltpu.SemaphoreType.DMA((4, rows // BLOCK)),
        ],
        compiler_params=params(dimension_semantics=("arbitrary",)),
        cost_estimate=cost(4e10 * cols / width, 1e8 * cols / width),
    )(meta, comb, h, w_down)


def final_kernel(own, shared, l0, l1, r0, r1, *refs):
    y = refs[-1]
    half = l0.shape[0]
    for i, (l, r) in enumerate(((l0, r0), (l1, r1))):
        rows = pl.ds(i * half, half)
        y[rows, :] = (own[rows, :] + shared[rows, :] + l[...].astype(F32) + r[...].astype(F32)).astype(BF16)


def final(own, shared, lefts, rights, y, start):
    tokens, cols = own.shape
    half = tokens // 2
    whole = pl.BlockSpec((tokens, cols), lambda i: (0, 0))
    part = pl.BlockSpec((half, cols), lambda i: (0, 0))
    place = pl.BlockSpec((tokens, cols), lambda i: (0, start // cols))
    before = () if y is None else (y,)
    return pl.pallas_call(
        final_kernel,
        grid=(1,),
        out_shape=jax.ShapeDtypeStruct(shared.shape, BF16),
        in_specs=[whole, place] + [part] * 4 + [ANY] * len(before),
        out_specs=place,
        input_output_aliases={6: 0} if before else {},
        compiler_params=params(),
        cost_estimate=cost(2e9, 8e6),
    )(own, shared, *lefts, *rights, *before)


def solution(mesh):
    ring = mesh.shape["ep"]
    assert ring == 4
    to_right = [(i, (i + 1) % ring) for i in range(ring)]
    to_left = [(i, (i - 1) % ring) for i in range(ring)]
    right = lambda v: lax.ppermute(v, "ep", to_right)
    left = lambda v: lax.ppermute(v, "ep", to_left)

    def tables(codes, n_experts, slots, slots_padded):
        expert, slot, gate = (codes[:, :, i] for i in range(3))
        tokens = expert.shape[2]
        here = expert - (lax.axis_index("ep") * n_experts).astype(F32)
        ids = lax.iota(jnp.int32, tokens)
        values = jnp.stack(
            [
                jnp.ones_like(gate),
                jnp.broadcast_to((ids // 128).astype(F32), gate.shape),
                jnp.broadcast_to((ids % 128).astype(F32), gate.shape),
                gate,
            ],
            axis=-1,
        ).astype(BF16)
        to_expert = (here[..., None] == lax.iota(jnp.int32, n_experts).astype(F32)).astype(BF16)
        lhs = (values[..., :, None] * to_expert[..., None, :]).reshape(*gate.shape, 4 * n_experts)
        cell = lax.iota(jnp.int32, slots_padded)
        to_slot = ((slot[..., None] == cell.astype(F32)) & (cell < slots)).astype(BF16)
        got = jnp.einsum("sjtc,sjtm->scm", to_slot, lhs, preferred_element_type=F32)
        used, high, low, weight = jnp.split(got, 4, axis=-1)
        token = jnp.where(used > 0.5, high * 128 + low, -1.0)
        last = jnp.max(jnp.where(used > 0.5, (cell + 1)[:, None], 0), axis=1)
        units = (last + UNIT - 1) // UNIT
        offset = jnp.cumsum(units, axis=1) - units
        total = jnp.sum(units, axis=0, keepdims=True)
        meta = jnp.concatenate([units, offset, total, jnp.cumsum(total, axis=1) - total]).astype(jnp.int32)
        tab = jnp.concatenate([token, weight], axis=-1)
        return meta, jnp.pad(tab, ((0, 0), (0, 0), (0, 128 - tab.shape[-1])))

    def step(x, expert, slot, gate, w_gate, w_up, w_down, s_gate, s_up, s_down):
        x = x[0, 0]
        tokens, width = x.shape
        top = expert.shape[-1]
        n_experts = w_gate.shape[0]
        slots = 5 * tokens * top // (4 * n_experts * ring)
        slots_padded = -(-slots // UNIT) * UNIT
        half = tokens // 2

        codes = jnp.stack(
            [
                expert[0, 0].astype(F32),
                jnp.minimum(slot[0, 0], slots).astype(F32),
                gate[0, 0].astype(BF16).astype(F32),
            ],
            axis=0,
        )
        codes = codes.transpose(2, 0, 1).astype(BF16)
        code_left, code_right = right(codes), left(codes)
        code_far = lax.ppermute(codes, "ep", [(i, (i + 2) % ring) for i in range(ring)])
        x_a, x_b = x[:half], x[half:]
        left_a, right_b = right(x_a), left(x_b)
        left_b, right_a = right(x_b), left(x_a)
        x_far = (right(left_a), left(right_b))

        codes = jnp.stack([codes, code_left, code_right, code_far]).astype(F32)
        meta, tab = tables(codes, n_experts, slots, slots_padded)

        g = jnp.dot(x, s_gate, preferred_element_type=F32)
        u = jnp.dot(x, s_up, preferred_element_type=F32)
        hidden = (jax.nn.silu(g) * u).astype(BF16)
        shared = jnp.dot(hidden, s_down, preferred_element_type=F32)

        meta, tab, shared = lax.optimization_barrier((meta, tab, shared))
        onehot, comb = build(meta, tab, tokens, slots_padded)
        zs = []
        for i, pieces in enumerate(((x,), (left_a, left_b), (right_a, right_b))):
            zs.append(dispatch(i, meta, onehot, pieces))
        h = gate_up(meta, onehot, zs, x_far, w_gate, w_up, slots_padded)

        y = None
        cols = width // CHUNKS
        for c in range(CHUNKS):
            start = c * cols
            own, left_sum, left_send, right_sum, right_send, far_a, far_b = down_combine(
                meta, comb, h, w_down, slots_padded, start, cols
            )
            from_left, from_right = right(far_a), left(far_b)
            lefts = [None, right(right_send)]
            rights = [left(left_send), None]
            lefts[0] = right((right_sum + from_left.astype(F32)).astype(BF16))
            rights[1] = left((left_sum + from_right.astype(F32)).astype(BF16))
            y = final(own, shared, lefts, rights, y, start)
        return y[None, None]

    token_spec = P("dp", "ep", None, None)
    weight_spec = P("ep", None, None)
    return jax.shard_map(
        step,
        mesh=mesh,
        in_specs=(token_spec,) * 4 + (weight_spec,) * 3 + (P(None, None),) * 3,
        out_specs=token_spec,
        check_vma=False,
    )
```

time: 1090 us -> 405 us (0.37)
  matrix products: 535 us -> 48.3 us
  blocking collectives: 263 us -> 0 us
  Pallas kernels: 0 us -> 203 us
  waiting for transfers between devices: 175 us -> 79 us
  local copies, waits for them, and re-layouts: 93 us -> 7.38 us
  starting transfers between devices: 8.39 us -> 57.5 us
    dot_general x9 -> x3, matrix products: 535 us -> 48.3 us  [the longest x1 31 us: step(): shared = jnp.dot(hidden, s_down, preferred_element_type=F32)]
    another operation x1 -> x0, blocking collectives: 263 us -> none  [placed(): return lax.with_sharding_constraint(v, NamedSharding(mesh, P(*spec)))]
    pallas_call x0 -> x13, Pallas kernels: none -> 203 us  [the longest x4 85.2 us: down_combine(): pl.pallas_call(functools.partial(down_kernel, n_experts, start), grid=(n_...]
    another operation x1 -> x0, waiting for transfers between devices: 175 us -> none  [placed(): return lax.with_sharding_constraint(v, NamedSharding(mesh, P(*spec)))]
    ppermute x0 -> x33, waiting for transfers between devices: none -> 79 us  [the longest x16 78.9 us: solution(): right = lambda v: lax.ppermute(v, 'ep', to_right)]
    another operation x3 -> x5, local copies, waits for them, and re-layouts: 71 us -> 0.14 us  [tables(): jnp.stack([jnp.ones_like(gate), jnp.broadcast_to((ids // 128).astype(F32)...]
    ppermute x0 -> x33, starting transfers between devices: none -> 57.5 us  [the longest x16 50 us: solution(): left = lambda v: lax.ppermute(v, 'ep', to_left)]
    convert_element_type x2 -> x0, local copies, waits for them, and re-layouts: 19.2 us -> none  [the longest x1 17.6 us: step(): einsum('abtke,abtkc->abtec', weighted, to_slot).astype(jnp.bfloat16)]
  transfers between devices with their start and end apart: 1 -> 33, of which waited for: 1 -> 11; matrix products, arithmetic and copies ran while one was open for 8% -> 14% of each run, Pallas kernels for 0% -> 16%
where the time goes in v1:
time: 405 us; the launch traced here: 400 us
  Pallas kernels  203 us (50%)
  waiting for transfers between devices  79 us (20%)
  starting transfers between devices  57.5 us (14%)
  matrix products  48.3 us (12%)
  local copies, waits for them, and re-layouts  7.38 us (2%)
  other arithmetic  4.41 us (1%)
    pallas_call x4, Pallas kernels, down_combine(): pl.pallas_call(functools.partial(down_kernel, n_experts, start), grid=(n_...  85.2 us
    ppermute x16, waiting for transfers between devices, solution(): right = lambda v: lax.ppermute(v, 'ep', to_right)  78.9 us
    pallas_call x1, Pallas kernels, gate_up(): pl.pallas_call(functools.partial(up_kernel, n_experts), grid=(n_experts,)...  72.7 us
    ppermute x16, starting transfers between devices, solution(): left = lambda v: lax.ppermute(v, 'ep', to_left)  50 us
    dot_general x1, matrix products, step(): shared = jnp.dot(hidden, s_down, preferred_element_type=F32)  31 us
    pallas_call x3, Pallas kernels, dispatch(): pl.pallas_call(functools.partial(dispatch_kernel, source, n_experts), out...  20.4 us
    dot_general x1, matrix products, step(): g = jnp.dot(x, s_gate, preferred_element_type=F32)  15.1 us
    pallas_call x4, Pallas kernels, final(): pl.pallas_call(final_kernel, grid=(1,), out_shape=jax.ShapeDtypeStruct(sh...  13.9 us
  transfers between devices with their start and end apart: 33, of which 11 were waited for; matrix products, arithmetic and copies ran while one was open for 14% of the time, Pallas kernels for 16%

profile of v1, /device:TPU:112, one launch (start us, length us, event | category | flops | bytes accessed | tf_op | source)
XLA Modules:
  0.0 400.2 jit_solution(84878746977644290)
XLA Ops:
  0.0 0.9 convert_element_type.148
  0.9 0.8 fusion.18
  1.7 4.0 collective-permute-start.1
  5.7 2.2 collective-permute-start.2
  7.9 4.0 slice_bitcast_fusion
  11.8 1.1 collective-permute-start.6
  12.9 0.9 collective-permute-start.4
  13.9 15.1 %fusion.35 = f32[768,2816]{1,0:T(8,128)} fusion(bf16[2048,2816]{1,0:T(8,128)(2,1)} %param.17, bf16[1,1,768,2048]{3,2,1,0:T(8,128)(2,1)S(1)} %copy-done), kind=kOutput, calls=%fused_computation.73 | convolution fusion | flops 8858370048 | bytes 23330816 | tf_op jit(solution)/shard_map/dot_general | solution.py:569
  29.0 31.0 %fusion.3.shared = f32[768,2048]{1,0:T(8,128)} fusion(bf16[2816,2048]{1,0:T(8,128)(2,1)} %param.19, f32[768,2816]{1,0:T(8,128)} %fusion.35, bf16[2048,2816]{1,0:T(8,128)(2,1)} %param.18, bf16[1,1,768,2048]{3,2,1,0:T(8,128)(2,1)S(1)} %copy-done), kind=kOutput, calls=%fused_computation.4 | convolution fusion | flops 17729716224 | bytes 41156608 | tf_op jit(solution)/shard_map/dot_general | solution.py:572
  60.0 2.4 collective-permute-start.5
  62.8 0.2 compare_convert_fusion
  62.9 0.2 broadcast_multiply_fusion
  63.1 2.3 fusion.8
  65.4 0.1 select_reduce_fusion
  65.6 0.2 reduce_window_sum.23
  65.8 0.2 reduce_window_sum.22
  66.1 0.7 pad.4.tab
  66.8 0.6 pad_add_fusion.meta
  67.4 3.2 collective-permute-start.8
  70.7 28.1 %collective-permute-done.3.refs_0_ = bf16[384,2048]{1,0:T(8,128)(2,1)} collective-permute-done((bf16[384,2048]{1,0:T(8,128)(2,1)}, bf16[384,2048]{1,0:T(8,128)(2,1)}, u32[]{:S(2)}, u32[]{:S(2)}) %collective-permute-start.3) | collective-permute-done | bytes 1572896 | tf_op jit(solution)/shard_map/ppermute | solution.py:509
  98.8 10.6 %build.1 = (bf16[4,6,256,768]{3,2,1,0:T(8,128)(2,1)}, bf16[4,6,768,256]{3,2,1,0:T(8,128)(2,1)}) custom-call(s32[10,16]{1,0:T(8,128)} %pad_add_fusion.meta, f32[4,96,128]{2,1,0:T(8,128)} %pad.4.tab), custom_call_target="tpu_custom_call" | custom-call | flops 15000000512 | bytes 20000000 | tf_op jit(solution)/shard_map/build/pallas_call | solution.py:90
  109.4 6.8 %shard_map.100.z0 = bf16[1536,2048]{1,0:T(8,128)(2,1)} custom-call(s32[10,16]{1,0:T(8,128)} %pad_add_fusion.meta, bf16[4,6,256,768]{3,2,1,0:T(8,128)(2,1)} %get-tuple-element.41.onehot, bf16[768,2048]{1,0:T(8,128)(2,1)} %bitcast.43), custom_call_target="tpu_custom_call" | custom-call | flops 5000000000 | bytes 8000000 | tf_op jit(solution)/shard_map/pallas_call | solution.py:167
  116.2 6.8 %shard_map.102.z2 = bf16[1536,2048]{1,0:T(8,128)(2,1)} custom-call(s32[10,16]{1,0:T(8,128)} %pad_add_fusion.meta, bf16[4,6,256,768]{3,2,1,0:T(8,128)(2,1)} %get-tuple-element.41.onehot, bf16[384,2048]{1,0:T(8,128)(2,1)} %collective-permute-done.5.refs_0_, bf16[384,2048]{1,0:T(8,128)(2,1)} %collective-permute-done.6.refs_1_), custom_call_target="tpu_custom_call" | custom-call | flops 5000000000 | bytes 8000000 | tf_op jit(solution)/shard_map/pallas_call | solution.py:167
  123.0 6.8 %shard_map.101.z1 = bf16[1536,2048]{1,0:T(8,128)(2,1)} custom-call(s32[10,16]{1,0:T(8,128)} %pad_add_fusion.meta, bf16[4,6,256,768]{3,2,1,0:T(8,128)(2,1)} %get-tuple-element.41.onehot, bf16[384,2048]{1,0:T(8,128)(2,1)} %collective-permute-done.3.refs_0_, bf16[384,2048]{1,0:T(8,128)(2,1)} %collective-permute-done.4.refs_1_), custom_call_target="tpu_custom_call" | custom-call | flops 5000000000 | bytes 8000000 | tf_op jit(solution)/shard_map/pallas_call | solution.py:167
  129.8 4.3 %collective-permute-done.7.x_a = bf16[384,2048]{1,0:T(8,128)(2,1)S(1)} collective-permute-done((bf16[384,2048]{1,0:T(8,128)(2,1)}, bf16[384,2048]{1,0:T(8,128)(2,1)S(1)}, u32[]{:S(2)}, u32[]{:S(2)}) %collective-permute-start.7) | collective-permute-done | bytes 1572896 | tf_op jit(solution)/shard_map/ppermute | solution.py:509
  134.1 1.1 copy-done.2
  135.3 72.7 %gate_up.1.h = bf16[6144,1408]{1,0:T(8,128)(2,1)} custom-call(s32[10,16]{1,0:T(8,128)} %pad_add_fusion.meta, bf16[4,6,256,768]{3,2,1,0:T(8,128)(2,1)} %get-tuple-element.41.onehot, bf16[1536,2048]{1,0:T(8,128)(2,1)} %shard_map.100.z0, bf16[1536,2048]{1,0:T(8,128)(2,1)} %shard_map.101.z1, bf16[1536,2048]{1,0:T(8,128)(2,1)} %shard_map.102.z2, ...), custom_call_target="tpu_custom_call" | custom-call | flops 60000002048 | bytes 200000000 | tf_op jit(solution)/shard_map/gate_up/pallas_call | solution.py:307
  208.0 21.3 %shard_map.106 = (f32[768,512]{1,0:T(8,128)}, f32[384,512]{1,0:T(8,128)}, bf16[384,512]{1,0:T(8,128)(2,1)}, f32[384,512]{1,0:T(8,128)}, bf16[384,512]{1,0:T(8,12...) custom-call(s32[10,16]{1,0:T(8,128)} %pad_add_fusion.meta, bf16[4,6,768,256]{3,2,1,0:T(8,128)(2,1)} %get-tuple-element.40.comb, ...), custom_call_target="tpu_custom_call" | custom-call | flops 10000000000 | bytes 25000000 | tf_op jit(solution)/shard_map/pallas_call | solution.py:455
  229.4 21.2 %shard_map.105 = (f32[768,512]{1,0:T(8,128)}, f32[384,512]{1,0:T(8,128)}, bf16[384,512]{1,0:T(8,128)(2,1)}, f32[384,512]{1,0:T(8,128)}, bf16[384,512]{1,0:T(8,12...) custom-call(s32[10,16]{1,0:T(8,128)} %pad_add_fusion.meta, bf16[4,6,768,256]{3,2,1,0:T(8,128)(2,1)} %get-tuple-element.40.comb, ...), custom_call_target="tpu_custom_call" | custom-call | flops 10000000000 | bytes 25000000 | tf_op jit(solution)/shard_map/pallas_call | solution.py:455
  250.6 21.3 %shard_map.104 = (f32[768,512]{1,0:T(8,128)}, f32[384,512]{1,0:T(8,128)}, bf16[384,512]{1,0:T(8,128)(2,1)}, f32[384,512]{1,0:T(8,128)}, bf16[384,512]{1,0:T(8,12...) custom-call(s32[10,16]{1,0:T(8,128)} %pad_add_fusion.meta, bf16[4,6,768,256]{3,2,1,0:T(8,128)(2,1)} %get-tuple-element.40.comb, ...), custom_call_target="tpu_custom_call" | custom-call | flops 10000000000 | bytes 25000000 | tf_op jit(solution)/shard_map/pallas_call | solution.py:455
  272.0 17.5 %collective-permute-start.31 = (bf16[384,512]{1,0:T(8,128)(2,1)}, bf16[384,512]{1,0:T(8,128)(2,1)S(1)}, u32[]{:S(2)}, u32[]{:S(2)}) collective-permute-start(bf16[384,512]{1,0:T(8,128)(2,1)} %get-tuple-element.70), channel_id=1, source_target_pairs={{0,3},{1,0},{2,1},{3,2},{4,7},{5,4},{6,5},{7,6},{8,11},{9,8},{10,9... | collective-permute-start | bytes 1179656 | tf_op jit(solution)/shard_map/ppermute | solution.py:510
  289.5 21.4 %shard_map.103 = (f32[768,512]{1,0:T(8,128)}, f32[384,512]{1,0:T(8,128)}, bf16[384,512]{1,0:T(8,128)(2,1)}, f32[384,512]{1,0:T(8,128)}, bf16[384,512]{1,0:T(8,12...) custom-call(s32[10,16]{1,0:T(8,128)} %pad_add_fusion.meta, bf16[4,6,768,256]{3,2,1,0:T(8,128)(2,1)} %get-tuple-element.40.comb, ...), custom_call_target="tpu_custom_call" | custom-call | flops 10000000000 | bytes 25000000 | tf_op jit(solution)/shard_map/pallas_call | solution.py:455
  311.1 4.1 %collective-permute-start.30 = (bf16[384,512]{1,0:T(8,128)(2,1)}, bf16[384,512]{1,0:T(8,128)(2,1)S(1)}, u32[]{:S(2)}, u32[]{:S(2)}) collective-permute-start(bf16[384,512]{1,0:T(8,128)(2,1)} %get-tuple-element.68), channel_id=1, source_target_pairs={{0,3},{1,0},{2,1},{3,2},{4,7},{5,4},{6,5},{7,6},{8,11},{9,8},{10,9... | collective-permute-start | bytes 1179656 | tf_op jit(solution)/shard_map/ppermute | solution.py:510
  315.2 1.3 collective-permute-start.23
  316.6 2.0 collective-permute-start.25
  318.8 6.5 %collective-permute-done.29.l1 = bf16[384,512]{1,0:T(8,128)(2,1)S(1)} collective-permute-done((bf16[384,512]{1,0:T(8,128)(2,1)}, bf16[384,512]{1,0:T(8,128)(2,1)S(1)}, u32[]{:S(2)}, u32[]{:S(2)}) %collective-permute-start.29) | collective-permute-done | bytes 393248 | tf_op jit(solution)/shard_map/ppermute | solution.py:509
  325.3 2.0 collective-permute-start.24
  327.3 6.4 %collective-permute-done.21 = bf16[384,512]{1,0:T(8,128)(2,1)S(1)} collective-permute-done((bf16[384,512]{1,0:T(8,128)(2,1)}, bf16[384,512]{1,0:T(8,128)(2,1)S(1)}, u32[]{:S(2)}, u32[]{:S(2)}) %collective-permute-start.21) | collective-permute-done | bytes 393248 | tf_op jit(solution)/shard_map/ppermute | solution.py:509
  333.7 0.1 add_convert_fusion.3
  333.9 3.3 collective-permute-start.19
  337.4 4.7 %collective-permute-done.23.l1 = bf16[384,512]{1,0:T(8,128)(2,1)S(1)} collective-permute-done((bf16[384,512]{1,0:T(8,128)(2,1)}, bf16[384,512]{1,0:T(8,128)(2,1)S(1)}, u32[]{:S(2)}, u32[]{:S(2)}) %collective-permute-start.23) | collective-permute-done | bytes 393248 | tf_op jit(solution)/shard_map/ppermute | solution.py:509
  342.1 2.0 collective-permute-start.18
  344.2 6.3 %collective-permute-done.15 = bf16[384,512]{1,0:T(8,128)(2,1)S(1)} collective-permute-done((bf16[384,512]{1,0:T(8,128)(2,1)S(1)}, bf16[384,512]{1,0:T(8,128)(2,1)S(1)}, u32[]{:S(2)}, u32[]{:S(2)}) %collective-permute-start.15) | collective-permute-done | bytes 393248 | tf_op jit(solution)/shard_map/ppermute | solution.py:509
  350.5 2.0 collective-permute-start.13
  352.9 6.0 %collective-permute-done.17.l1 = bf16[384,512]{1,0:T(8,128)(2,1)S(1)} collective-permute-done((bf16[384,512]{1,0:T(8,128)(2,1)S(1)}, bf16[384,512]{1,0:T(8,128)(2,1)S(1)}, u32[]{:S(2)}, u32[]{:S(2)}) %collective-permute-start.17) | collective-permute-done | bytes 393248 | tf_op jit(solution)/shard_map/ppermute | solution.py:509
  359.0 2.0 collective-permute-start.32
  361.0 6.4 %collective-permute-done.9 = bf16[384,512]{1,0:T(8,128)(2,1)S(1)} collective-permute-done((bf16[384,512]{1,0:T(8,128)(2,1)S(1)}, bf16[384,512]{1,0:T(8,128)(2,1)S(1)}, u32[]{:S(2)}, u32[]{:S(2)}) %collective-permute-start.9) | collective-permute-done | bytes 393248 | tf_op jit(solution)/shard_map/ppermute | solution.py:509
  367.4 2.0 collective-permute-start.26
  369.6 6.1 %collective-permute-done.28.l0 = bf16[384,512]{1,0:T(8,128)(2,1)S(1)} collective-permute-done((bf16[384,512]{1,0:T(8,128)(2,1)S(1)}, bf16[384,512]{1,0:T(8,128)(2,1)S(1)}, u32[]{:S(2)}, u32[]{:S(2)}) %collective-permute-start.28) | collective-permute-done | bytes 393248 | tf_op jit(solution)/shard_map/ppermute | solution.py:509
  375.6 0.8 collective-permute-start.20
  376.6 1.3 collective-permute-start.11
  377.9 1.9 collective-permute-done.22.l0
  379.8 0.8 collective-permute-start.12
  380.6 1.2 collective-permute-start.10
  381.9 2.2 collective-permute-done.16.l0
  384.1 0.8 collective-permute-start.14
  384.9 3.5 shard_map.107.refs_0_
  388.4 3.5 shard_map.108.refs_0_
  391.9 3.5 shard_map.109.refs_0_
  395.4 0.7 copy-done.20
  396.1 0.2 copy-done.23
  396.2 0.1 copy-done.24
  396.4 0.2 copy-done.25
  396.6 3.5 shard_map.110
  (122 shorter events, 2.1 us)
Async XLA Ops:
  0.0 13.9 %copy-start = (bf16[1,1,768,2048]{3,2,1,0:T(8,128)(2,1)S(1)}, bf16[1,1,768,2048]{3,2,1,0:T(8,128)(2,1)}, u32[]{:S(2)}) copy-start(bf16[1,1,768,2048]{3,2,1,0:T(8,128)(2,1)} %param.10) | copy-start | bytes 9437188
  1.7 58.3 %collective-permute-start.1 = (bf16[6,3,768]{2,0,1:T(8,128)(2,1)S(1)}, bf16[6,3,768]{2,0,1:T(8,128)(2,1)S(1)}, u32[]{:S(2)}, u32[]{:S(2)}) collective-permute-start(bf16[6,3,768]{2,0,1:T(8,128)(2,1)S(1)} %get-tuple-element.83), channel_id=1, source_target_pairs={{0,3},{1,0},{2,1},{3,2},{4,7},{5,4},{6,5},{7,6},{8,11},{9,8},{10,9... | collective-permute-start | bytes 82952 | tf_op jit(solution)/shard_map/ppermute | solution.py:510
  5.7 56.7 %collective-permute-start = (bf16[6,3,768]{2,0,1:T(8,128)(2,1)S(1)}, bf16[6,3,768]{2,0,1:T(8,128)(2,1)S(1)}, u32[]{:S(2)}, u32[]{:S(2)}) collective-permute-start(bf16[6,3,768]{2,0,1:T(8,128)(2,1)S(1)} %get-tuple-element.83), channel_id=1, source_target_pairs={{0,1},{1,2},{2,3},{3,0},{4,5},{5,6},{6,7},{7,4},{8,9},{9,10},{10,1... | collective-permute-start | bytes 82952 | tf_op jit(solution)/shard_map/ppermute | solution.py:509
  5.7 56.7 %collective-permute-start.2 = (bf16[6,3,768]{2,0,1:T(8,128)(2,1)S(1)}, bf16[6,3,768]{2,0,1:T(8,128)(2,1)S(1)}, u32[]{:S(2)}, u32[]{:S(2)}) collective-permute-start(bf16[6,3,768]{2,0,1:T(8,128)(2,1)S(1)} %get-tuple-element.83), channel_id=1, source_target_pairs={{0,2},{1,3},{2,0},{3,1},{4,6},{5,7},{6,4},{7,5},{8,10},{9,11},{10,... | collective-permute-start | bytes 82952 | tf_op jit(solution)/shard_map/ppermute | solution.py:560
  11.8 55.6 %collective-permute-start.6 = (bf16[384,2048]{1,0:T(8,128)(2,1)}, bf16[384,2048]{1,0:T(8,128)(2,1)}, u32[]{:S(2)}, u32[]{:S(2)}) collective-permute-start(bf16[384,2048]{1,0:T(8,128)(2,1)} %get-tuple-element.75), channel_id=1, source_target_pairs={{0,3},{1,0},{2,1},{3,2},{4,7},{5,4},{6,5},{7,6},{8,11},{9,8},{10,9... | collective-permute-start | bytes 4718600 | tf_op jit(solution)/shard_map/ppermute | solution.py:510
  12.9 110.0 %collective-permute-start.4 = (bf16[384,2048]{1,0:T(8,128)(2,1)}, bf16[384,2048]{1,0:T(8,128)(2,1)}, u32[]{:S(2)}, u32[]{:S(2)}) collective-permute-start(bf16[384,2048]{1,0:T(8,128)(2,1)} %get-tuple-element.75), channel_id=1, source_target_pairs={{0,1},{1,2},{2,3},{3,0},{4,5},{5,6},{6,7},{7,4},{8,9},{9,10},{10,1... | collective-permute-start | bytes 4718600 | tf_op jit(solution)/shard_map/ppermute | solution.py:509
  60.0 56.1 %collective-permute-start.5 = (bf16[384,2048]{1,0:T(8,128)(2,1)}, bf16[384,2048]{1,0:T(8,128)(2,1)}, u32[]{:S(2)}, u32[]{:S(2)}) collective-permute-start(bf16[384,2048]{1,0:T(8,128)(2,1)} %get-tuple-element.76), channel_id=1, source_target_pairs={{0,3},{1,0},{2,1},{3,2},{4,7},{5,4},{6,5},{7,6},{8,11},{9,8},{10,9... | collective-permute-start | bytes 4718600 | tf_op jit(solution)/shard_map/ppermute | solution.py:510
  62.4 36.3 %collective-permute-start.3 = (bf16[384,2048]{1,0:T(8,128)(2,1)}, bf16[384,2048]{1,0:T(8,128)(2,1)}, u32[]{:S(2)}, u32[]{:S(2)}) collective-permute-start(bf16[384,2048]{1,0:T(8,128)(2,1)} %get-tuple-element.76), channel_id=1, source_target_pairs={{0,1},{1,2},{2,3},{3,0},{4,5},{5,6},{6,7},{7,4},{8,9},{9,10},{10,1... | collective-permute-start | bytes 4718600 | tf_op jit(solution)/shard_map/ppermute | solution.py:509
  67.4 62.4 %collective-permute-start.8 = (bf16[384,2048]{1,0:T(8,128)(2,1)}, bf16[384,2048]{1,0:T(8,128)(2,1)S(1)}, u32[]{:S(2)}, u32[]{:S(2)}) collective-permute-start(bf16[384,2048]{1,0:T(8,128)(2,1)} %collective-permute-done.6.refs_1_), channel_id=1, source_target_pairs={{0,3},{1,0},{2,1},{3,2},{4,7},{5,4},{6,5},{7,6},{8,11},{9,8},{10,9... | collective-permute-start | bytes 4718600 | tf_op jit(solution)/shard_map/ppermute | solution.py:510
  98.7 35.4 %collective-permute-start.7 = (bf16[384,2048]{1,0:T(8,128)(2,1)}, bf16[384,2048]{1,0:T(8,128)(2,1)S(1)}, u32[]{:S(2)}, u32[]{:S(2)}) collective-permute-start(bf16[384,2048]{1,0:T(8,128)(2,1)} %collective-permute-done.3.refs_0_), channel_id=1, source_target_pairs={{0,1},{1,2},{2,3},{3,0},{4,5},{5,6},{6,7},{7,4},{8,9},{9,10},{10,1... | collective-permute-start | bytes 4718600 | tf_op jit(solution)/shard_map/ppermute | solution.py:509
  129.8 4.3 %copy-start.1 = (bf16[384,2048]{1,0:T(8,128)(2,1)}, bf16[384,2048]{1,0:T(8,128)(2,1)S(1)}, u32[]{:S(2)}) copy-start(bf16[384,2048]{1,0:T(8,128)(2,1)S(1)} %collective-permute-done.8.x_b) | copy-start | bytes 4718596
  134.1 1.1 copy-start.2
  271.9 43.3 %collective-permute-start.27 = (bf16[384,512]{1,0:T(8,128)(2,1)}, bf16[384,512]{1,0:T(8,128)(2,1)S(1)}, u32[]{:S(2)}, u32[]{:S(2)}) collective-permute-start(bf16[384,512]{1,0:T(8,128)(2,1)} %get-tuple-element.66), channel_id=1, source_target_pairs={{0,1},{1,2},{2,3},{3,0},{4,5},{5,6},{6,7},{7,4},{8,9},{9,10},{10,1... | collective-permute-start | bytes 1179656 | tf_op jit(solution)/shard_map/ppermute | solution.py:509
  272.0 44.5 %copy-start.10 = (f32[384,512]{1,0:T(8,128)S(1)}, f32[384,512]{1,0:T(8,128)}, u32[]{:S(2)}) copy-start(f32[384,512]{1,0:T(8,128)} %get-tuple-element.65) | copy-start | bytes 2359300
  272.0 46.7 %copy-start.9 = (f32[384,512]{1,0:T(8,128)S(1)}, f32[384,512]{1,0:T(8,128)}, u32[]{:S(2)}) copy-start(f32[384,512]{1,0:T(8,128)} %get-tuple-element.69) | copy-start | bytes 2359300
  272.0 61.7 %copy-start.31 = (bf16[384,512]{1,0:T(8,128)(2,1)S(1)}, bf16[384,512]{1,0:T(8,128)(2,1)}, u32[]{:S(2)}) copy-start(bf16[384,512]{1,0:T(8,128)(2,1)} %get-tuple-element.52) | copy-start | bytes 1179652
  272.0 61.7 %copy-start.8 = (f32[384,512]{1,0:T(8,128)S(1)}, f32[384,512]{1,0:T(8,128)}, u32[]{:S(2)}) copy-start(f32[384,512]{1,0:T(8,128)} %get-tuple-element.58) | copy-start | bytes 2359300
  272.0 44.6 %collective-permute-start.31 = (bf16[384,512]{1,0:T(8,128)(2,1)}, bf16[384,512]{1,0:T(8,128)(2,1)S(1)}, u32[]{:S(2)}, u32[]{:S(2)}) collective-permute-start(bf16[384,512]{1,0:T(8,128)(2,1)} %get-tuple-element.70), channel_id=1, source_target_pairs={{0,3},{1,0},{2,1},{3,2},{4,7},{5,4},{6,5},{7,6},{8,11},{9,8},{10,9... | collective-permute-start | bytes 1179656 | tf_op jit(solution)/shard_map/ppermute | solution.py:510
  310.9 23.0 %copy-start.30 = (bf16[384,512]{1,0:T(8,128)(2,1)S(1)}, bf16[384,512]{1,0:T(8,128)(2,1)}, u32[]{:S(2)}) copy-start(bf16[384,512]{1,0:T(8,128)(2,1)} %get-tuple-element.56) | copy-start | bytes 1179652
  310.9 26.3 %copy-start.7 = (f32[384,512]{1,0:T(8,128)S(1)}, f32[384,512]{1,0:T(8,128)}, u32[]{:S(2)}) copy-start(f32[384,512]{1,0:T(8,128)} %get-tuple-element.62) | copy-start | bytes 2359300
  310.9 26.4 %copy-start.29 = (bf16[384,512]{1,0:T(8,128)(2,1)S(1)}, bf16[384,512]{1,0:T(8,128)(2,1)}, u32[]{:S(2)}) copy-start(bf16[384,512]{1,0:T(8,128)(2,1)} %get-tuple-element.53) | copy-start | bytes 1179652
  310.9 31.2 %copy-start.27 = (bf16[384,512]{1,0:T(8,128)(2,1)S(1)}, bf16[384,512]{1,0:T(8,128)(2,1)}, u32[]{:S(2)}) copy-start(bf16[384,512]{1,0:T(8,128)(2,1)} %get-tuple-element.54) | copy-start | bytes 1179652
  310.9 33.2 %copy-start.28 = (bf16[384,512]{1,0:T(8,128)(2,1)S(1)}, bf16[384,512]{1,0:T(8,128)(2,1)}, u32[]{:S(2)}) copy-start(bf16[384,512]{1,0:T(8,128)(2,1)} %get-tuple-element.45) | copy-start | bytes 1179652
  310.9 39.6 %copy-start.26 = (bf16[384,512]{1,0:T(8,128)(2,1)S(1)}, bf16[384,512]{1,0:T(8,128)(2,1)}, u32[]{:S(2)}) copy-start(bf16[384,512]{1,0:T(8,128)(2,1)} %get-tuple-element.49) | copy-start | bytes 1179652
  310.9 41.6 %copy-start.6 = (f32[384,512]{1,0:T(8,128)S(1)}, f32[384,512]{1,0:T(8,128)}, u32[]{:S(2)}) copy-start(f32[384,512]{1,0:T(8,128)} %get-tuple-element.51) | copy-start | bytes 2359300
  311.0 41.8 %copy-start.5 = (f32[384,512]{1,0:T(8,128)S(1)}, f32[384,512]{1,0:T(8,128)}, u32[]{:S(2)}) copy-start(f32[384,512]{1,0:T(8,128)} %get-tuple-element.55) | copy-start | bytes 2359300
  311.0 14.3 %collective-permute-start.29 = (bf16[384,512]{1,0:T(8,128)(2,1)}, bf16[384,512]{1,0:T(8,128)(2,1)S(1)}, u32[]{:S(2)}, u32[]{:S(2)}) collective-permute-start(bf16[384,512]{1,0:T(8,128)(2,1)} %get-tuple-element.67), channel_id=1, source_target_pairs={{0,1},{1,2},{2,3},{3,0},{4,5},{5,6},{6,7},{7,4},{8,9},{9,10},{10,1... | collective-permute-start | bytes 1179656 | tf_op jit(solution)/shard_map/ppermute | solution.py:509
  311.1 26.2 %collective-permute-start.30 = (bf16[384,512]{1,0:T(8,128)(2,1)}, bf16[384,512]{1,0:T(8,128)(2,1)S(1)}, u32[]{:S(2)}, u32[]{:S(2)}) collective-permute-start(bf16[384,512]{1,0:T(8,128)(2,1)} %get-tuple-element.68), channel_id=1, source_target_pairs={{0,3},{1,0},{2,1},{3,2},{4,7},{5,4},{6,5},{7,6},{8,11},{9,8},{10,9... | collective-permute-start | bytes 1179656 | tf_op jit(solution)/shard_map/ppermute | solution.py:510
  315.2 18.5 %collective-permute-start.21 = (bf16[384,512]{1,0:T(8,128)(2,1)}, bf16[384,512]{1,0:T(8,128)(2,1)S(1)}, u32[]{:S(2)}, u32[]{:S(2)}) collective-permute-start(bf16[384,512]{1,0:T(8,128)(2,1)} %get-tuple-element.59), channel_id=1, source_target_pairs={{0,1},{1,2},{2,3},{3,0},{4,5},{5,6},{6,7},{7,4},{8,9},{9,10},{10,1... | collective-permute-start | bytes 1179656 | tf_op jit(solution)/shard_map/ppermute | solution.py:509
  315.2 26.9 %collective-permute-start.23 = (bf16[384,512]{1,0:T(8,128)(2,1)}, bf16[384,512]{1,0:T(8,128)(2,1)S(1)}, u32[]{:S(2)}, u32[]{:S(2)}) collective-permute-start(bf16[384,512]{1,0:T(8,128)(2,1)} %get-tuple-element.60), channel_id=1, source_target_pairs={{0,1},{1,2},{2,3},{3,0},{4,5},{5,6},{6,7},{7,4},{8,9},{9,10},{10,1... | collective-permute-start | bytes 1179656 | tf_op jit(solution)/shard_map/ppermute | solution.py:509
  316.6 52.8 %copy-start.4 = (f32[384,512]{1,0:T(8,128)S(1)}, f32[384,512]{1,0:T(8,128)}, u32[]{:S(2)}) copy-start(f32[384,512]{1,0:T(8,128)} %get-tuple-element.44) | copy-start | bytes 2359300
  316.6 17.2 %collective-permute-start.25 = (bf16[384,512]{1,0:T(8,128)(2,1)}, bf16[384,512]{1,0:T(8,128)(2,1)S(1)}, u32[]{:S(2)}, u32[]{:S(2)}) collective-permute-start(bf16[384,512]{1,0:T(8,128)(2,1)} %get-tuple-element.63), channel_id=1, source_target_pairs={{0,3},{1,0},{2,1},{3,2},{4,7},{5,4},{6,5},{7,6},{8,11},{9,8},{10,9... | collective-permute-start | bytes 1179656 | tf_op jit(solution)/shard_map/ppermute | solution.py:510
  318.8 57.6 %copy-start.3 = (f32[384,512]{1,0:T(8,128)S(1)}, f32[384,512]{1,0:T(8,128)}, u32[]{:S(2)}) copy-start(f32[384,512]{1,0:T(8,128)} %get-tuple-element.48) | copy-start | bytes 2359300
  325.3 51.3 %copy-start.11 = (bf16[384,512]{1,0:T(8,128)(2,1)}, bf16[384,512]{1,0:T(8,128)(2,1)S(1)}, u32[]{:S(2)}) copy-start(bf16[384,512]{1,0:T(8,128)(2,1)S(1)} %collective-permute-done.29.l1) | copy-start | bytes 1179652
  325.3 18.9 %collective-permute-start.24 = (bf16[384,512]{1,0:T(8,128)(2,1)}, bf16[384,512]{1,0:T(8,128)(2,1)S(1)}, u32[]{:S(2)}, u32[]{:S(2)}) collective-permute-start(bf16[384,512]{1,0:T(8,128)(2,1)} %get-tuple-element.61), channel_id=1, source_target_pairs={{0,3},{1,0},{2,1},{3,2},{4,7},{5,4},{6,5},{7,6},{8,11},{9,8},{10,9... | collective-permute-start | bytes 1179656 | tf_op jit(solution)/shard_map/ppermute | solution.py:510
  333.7 16.9 %collective-permute-start.15 = (bf16[384,512]{1,0:T(8,128)(2,1)S(1)}, bf16[384,512]{1,0:T(8,128)(2,1)S(1)}, u32[]{:S(2)}, u32[]{:S(2)}) collective-permute-start(bf16[384,512]{1,0:T(8,128)(2,1)S(1)} %copy-done.31), channel_id=1, source_target_pairs={{0,1},{1,2},{2,3},{3,0},{4,5},{5,6},{6,7},{7,4},{8,9},{9,10},{10,1... | collective-permute-start | bytes 1179656 | tf_op jit(solution)/shard_map/ppermute | solution.py:509
  333.9 18.8 %collective-permute-start.19 = (bf16[384,512]{1,0:T(8,128)(2,1)S(1)}, bf16[384,512]{1,0:T(8,128)(2,1)S(1)}, u32[]{:S(2)}, u32[]{:S(2)}) collective-permute-start(bf16[384,512]{1,0:T(8,128)(2,1)S(1)} %copy-done.30), channel_id=1, source_target_pairs={{0,3},{1,0},{2,1},{3,2},{4,7},{5,4},{6,5},{7,6},{8,11},{9,8},{10,9... | collective-permute-start | bytes 1179656 | tf_op jit(solution)/shard_map/ppermute | solution.py:510
  337.3 47.6 %copy-start.12 = (bf16[384,512]{1,0:T(8,128)(2,1)}, bf16[384,512]{1,0:T(8,128)(2,1)S(1)}, u32[]{:S(2)}) copy-start(bf16[384,512]{1,0:T(8,128)(2,1)S(1)} %collective-permute-done.30.r0) | copy-start | bytes 1179652
  337.3 21.7 %collective-permute-start.17 = (bf16[384,512]{1,0:T(8,128)(2,1)S(1)}, bf16[384,512]{1,0:T(8,128)(2,1)S(1)}, u32[]{:S(2)}, u32[]{:S(2)}) collective-permute-start(bf16[384,512]{1,0:T(8,128)(2,1)S(1)} %copy-done.29), channel_id=1, source_target_pairs={{0,1},{1,2},{2,3},{3,0},{4,5},{5,6},{6,7},{7,4},{8,9},{9,10},{10,1... | collective-permute-start | bytes 1179656 | tf_op jit(solution)/shard_map/ppermute | solution.py:509
  342.1 42.7 %copy-start.15 = (bf16[384,512]{1,0:T(8,128)(2,1)}, bf16[384,512]{1,0:T(8,128)(2,1)S(1)}, u32[]{:S(2)}) copy-start(bf16[384,512]{1,0:T(8,128)(2,1)S(1)} %collective-permute-done.23.l1) | copy-start | bytes 1179652
  342.1 18.9 %collective-permute-start.18 = (bf16[384,512]{1,0:T(8,128)(2,1)S(1)}, bf16[384,512]{1,0:T(8,128)(2,1)S(1)}, u32[]{:S(2)}, u32[]{:S(2)}) collective-permute-start(bf16[384,512]{1,0:T(8,128)(2,1)S(1)} %copy-done.27), channel_id=1, source_target_pairs={{0,3},{1,0},{2,1},{3,2},{4,7},{5,4},{6,5},{7,6},{8,11},{9,8},{10,9... | collective-permute-start | bytes 1179656 | tf_op jit(solution)/shard_map/ppermute | solution.py:510
  344.1 40.7 %copy-start.16 = (bf16[384,512]{1,0:T(8,128)(2,1)}, bf16[384,512]{1,0:T(8,128)(2,1)S(1)}, u32[]{:S(2)}) copy-start(bf16[384,512]{1,0:T(8,128)(2,1)S(1)} %collective-permute-done.24.r0) | copy-start | bytes 1179652
  344.1 23.3 %collective-permute-start.9 = (bf16[384,512]{1,0:T(8,128)(2,1)S(1)}, bf16[384,512]{1,0:T(8,128)(2,1)S(1)}, u32[]{:S(2)}, u32[]{:S(2)}) collective-permute-start(bf16[384,512]{1,0:T(8,128)(2,1)S(1)} %copy-done.28), channel_id=1, source_target_pairs={{0,1},{1,2},{2,3},{3,0},{4,5},{5,6},{6,7},{7,4},{8,9},{9,10},{10,1... | collective-permute-start | bytes 1179656 | tf_op jit(solution)/shard_map/ppermute | solution.py:509
  350.5 18.9 %collective-permute-start.13 = (bf16[384,512]{1,0:T(8,128)(2,1)S(1)}, bf16[384,512]{1,0:T(8,128)(2,1)S(1)}, u32[]{:S(2)}, u32[]{:S(2)}) collective-permute-start(bf16[384,512]{1,0:T(8,128)(2,1)S(1)} %copy-done.26), channel_id=1, source_target_pairs={{0,3},{1,0},{2,1},{3,2},{4,7},{5,4},{6,5},{7,6},{8,11},{9,8},{10,9... | collective-permute-start | bytes 1179656 | tf_op jit(solution)/shard_map/ppermute | solution.py:510
  352.7 22.9 %collective-permute-start.28 = (bf16[384,512]{1,0:T(8,128)(2,1)S(1)}, bf16[384,512]{1,0:T(8,128)(2,1)S(1)}, u32[]{:S(2)}, u32[]{:S(2)}) collective-permute-start(bf16[384,512]{1,0:T(8,128)(2,1)S(1)} %add_convert_fusion.1), channel_id=1, source_target_pairs={{0,1},{1,2},{2,3},{3,0},{4,5},{5,6},{6,7},{7,4},{8,9},{9,10},{10,1... | collective-permute-start | bytes 1179656 | tf_op jit(solution)/shard_map/ppermute | solution.py:509
  359.0 25.9 %copy-start.17 = (bf16[384,512]{1,0:T(8,128)(2,1)}, bf16[384,512]{1,0:T(8,128)(2,1)S(1)}, u32[]{:S(2)}) copy-start(bf16[384,512]{1,0:T(8,128)(2,1)S(1)} %collective-permute-done.17.l1) | copy-start | bytes 1179652
  359.0 17.6 %collective-permute-start.32 = (bf16[384,512]{1,0:T(8,128)(2,1)S(1)}, bf16[384,512]{1,0:T(8,128)(2,1)S(1)}, u32[]{:S(2)}, u32[]{:S(2)}) collective-permute-start(bf16[384,512]{1,0:T(8,128)(2,1)S(1)} %add_convert_fusion), channel_id=1, source_target_pairs={{0,3},{1,0},{2,1},{3,2},{4,7},{5,4},{6,5},{7,6},{8,11},{9,8},{10,9... | collective-permute-start | bytes 1179656 | tf_op jit(solution)/shard_map/ppermute | solution.py:510
  361.0 23.9 %copy-start.18 = (bf16[384,512]{1,0:T(8,128)(2,1)}, bf16[384,512]{1,0:T(8,128)(2,1)S(1)}, u32[]{:S(2)}) copy-start(bf16[384,512]{1,0:T(8,128)(2,1)S(1)} %collective-permute-done.18.r0) | copy-start | bytes 1179652
  361.0 18.9 %collective-permute-start.22 = (bf16[384,512]{1,0:T(8,128)(2,1)S(1)}, bf16[384,512]{1,0:T(8,128)(2,1)S(1)}, u32[]{:S(2)}, u32[]{:S(2)}) collective-permute-start(bf16[384,512]{1,0:T(8,128)(2,1)S(1)} %add_convert_fusion.3), channel_id=1, source_target_pairs={{0,1},{1,2},{2,3},{3,0},{4,5},{5,6},{6,7},{7,4},{8,9},{9,10},{10,1... | collective-permute-start | bytes 1179656 | tf_op jit(solution)/shard_map/ppermute | solution.py:509
  367.4 13.2 %collective-permute-start.26 = (bf16[384,512]{1,0:T(8,128)(2,1)S(1)}, bf16[384,512]{1,0:T(8,128)(2,1)S(1)}, u32[]{:S(2)}, u32[]{:S(2)}) collective-permute-start(bf16[384,512]{1,0:T(8,128)(2,1)S(1)} %add_convert_fusion.2), channel_id=1, source_target_pairs={{0,3},{1,0},{2,1},{3,2},{4,7},{5,4},{6,5},{7,6},{8,11},{9,8},{10,9... | collective-permute-start | bytes 1179656 | tf_op jit(solution)/shard_map/ppermute | solution.py:510
  369.4 14.6 %collective-permute-start.16 = (bf16[384,512]{1,0:T(8,128)(2,1)S(1)}, bf16[384,512]{1,0:T(8,128)(2,1)S(1)}, u32[]{:S(2)}, u32[]{:S(2)}) collective-permute-start(bf16[384,512]{1,0:T(8,128)(2,1)S(1)} %add_convert_fusion.5), channel_id=1, source_target_pairs={{0,1},{1,2},{2,3},{3,0},{4,5},{5,6},{6,7},{7,4},{8,9},{9,10},{10,1... | collective-permute-start | bytes 1179656 | tf_op jit(solution)/shard_map/ppermute | solution.py:509
  375.6 9.3 %copy-start.13 = (bf16[384,512]{1,0:T(8,128)(2,1)}, bf16[384,512]{1,0:T(8,128)(2,1)S(1)}, u32[]{:S(2)}) copy-start(bf16[384,512]{1,0:T(8,128)(2,1)S(1)} %collective-permute-done.28.l0) | copy-start | bytes 1179652
  375.6 16.2 %collective-permute-start.20 = (bf16[384,512]{1,0:T(8,128)(2,1)S(1)}, bf16[384,512]{1,0:T(8,128)(2,1)}, u32[]{:S(2)}, u32[]{:S(2)}) collective-permute-start(bf16[384,512]{1,0:T(8,128)(2,1)S(1)} %add_convert_fusion.4), channel_id=1, source_target_pairs={{0,3},{1,0},{2,1},{3,2},{4,7},{5,4},{6,5},{7,6},{8,11},{9,8},{10,9... | collective-permute-start | bytes 1179656 | tf_op jit(solution)/shard_map/ppermute | solution.py:510
  376.6 8.3 %copy-start.14 = (bf16[384,512]{1,0:T(8,128)(2,1)}, bf16[384,512]{1,0:T(8,128)(2,1)S(1)}, u32[]{:S(2)}) copy-start(bf16[384,512]{1,0:T(8,128)(2,1)S(1)} %collective-permute-done.32.r1) | copy-start | bytes 1179652
  376.6 18.7 %collective-permute-start.11 = (bf16[384,512]{1,0:T(8,128)(2,1)}, bf16[384,512]{1,0:T(8,128)(2,1)S(1)}, u32[]{:S(2)}, u32[]{:S(2)}) collective-permute-start(bf16[384,512]{1,0:T(8,128)(2,1)} %get-tuple-element.46), channel_id=1, source_target_pairs={{0,1},{1,2},{2,3},{3,0},{4,5},{5,6},{6,7},{7,4},{8,9},{9,10},{10,1... | collective-permute-start | bytes 1179656 | tf_op jit(solution)/shard_map/ppermute | solution.py:509
  379.8 5.0 %copy-start.19 = (bf16[384,512]{1,0:T(8,128)(2,1)}, bf16[384,512]{1,0:T(8,128)(2,1)S(1)}, u32[]{:S(2)}) copy-start(bf16[384,512]{1,0:T(8,128)(2,1)S(1)} %collective-permute-done.22.l0) | copy-start | bytes 1179652
  379.8 15.5 %collective-permute-start.12 = (bf16[384,512]{1,0:T(8,128)(2,1)}, bf16[384,512]{1,0:T(8,128)(2,1)S(1)}, u32[]{:S(2)}, u32[]{:S(2)}) collective-permute-start(bf16[384,512]{1,0:T(8,128)(2,1)} %get-tuple-element.47), channel_id=1, source_target_pairs={{0,3},{1,0},{2,1},{3,2},{4,7},{5,4},{6,5},{7,6},{8,11},{9,8},{10,9... | collective-permute-start | bytes 1179656 | tf_op jit(solution)/shard_map/ppermute | solution.py:510
  380.6 4.2 %copy-start.22 = (bf16[384,512]{1,0:T(8,128)(2,1)}, bf16[384,512]{1,0:T(8,128)(2,1)S(1)}, u32[]{:S(2)}) copy-start(bf16[384,512]{1,0:T(8,128)(2,1)S(1)} %collective-permute-done.26.r1) | copy-start | bytes 1179652
  380.6 14.7 %collective-permute-start.10 = (bf16[384,512]{1,0:T(8,128)(2,1)S(1)}, bf16[384,512]{1,0:T(8,128)(2,1)S(1)}, u32[]{:S(2)}, u32[]{:S(2)}) collective-permute-start(bf16[384,512]{1,0:T(8,128)(2,1)S(1)} %add_convert_fusion.7), channel_id=1, source_target_pairs={{0,1},{1,2},{2,3},{3,0},{4,5},{5,6},{6,7},{7,4},{8,9},{9,10},{10,1... | collective-permute-start | bytes 1179656 | tf_op jit(solution)/shard_map/ppermute | solution.py:509
  384.1 0.8 copy-start.21
  384.1 11.3 %collective-permute-start.14 = (bf16[384,512]{1,0:T(8,128)(2,1)S(1)}, bf16[384,512]{1,0:T(8,128)(2,1)S(1)}, u32[]{:S(2)}, u32[]{:S(2)}) collective-permute-start(bf16[384,512]{1,0:T(8,128)(2,1)S(1)} %add_convert_fusion.6), channel_id=1, source_target_pairs={{0,3},{1,0},{2,1},{3,2},{4,7},{5,4},{6,5},{7,6},{8,11},{9,8},{10,9... | collective-permute-start | bytes 1179656 | tf_op jit(solution)/shard_map/ppermute | solution.py:510
  395.3 0.9 copy-start.23
  395.4 1.0 copy-start.24
  395.4 1.2 copy-start.25
  (1 other events, 0.8 us)

commit v2 on v1

--- a/solution.py
+++ b/solution.py
@@ -8,7 +8,7 @@
 from jax.sharding import PartitionSpec as P
 
 
-CHUNKS = 4
+CHUNKS = (3, 3, 2)
 UNIT = 16
 BLOCK = 256
 F32, BF16 = jnp.float32, jnp.bfloat16
@@ -186,9 +186,9 @@
     return [m for m in (128, 256) if m < limit] + [limit]
 
 
-def for_rows(rows, limit, body):
+def for_rows(rows, limit, body, among=None):
     low = 0
-    for m in sizes(limit):
+    for m in among or sizes(limit):
         pl.when((rows > low) & (rows <= m))(functools.partial(body, m))
         low = m
 
@@ -340,6 +340,7 @@
     tokens = acc.shape[0]
     half = tokens // 2
     per = BLOCK // UNIT
+    fine = [*range(64, most, 64), most]
 
     def unit(i):
         return pl.ds(pl.multiple_of(i * UNIT, UNIT), UNIT)
@@ -361,7 +362,7 @@
         return pltpu.make_async_copy(wd.at[e, :, pl.ds(start, cols)], wbuf.at[i], w_sem.at[i])
 
     def load(e):
-        for_rows(meta[8, e] * UNIT, most, lambda m: in_copy(e, m).start())
+        for_rows(meta[8, e] * UNIT, most, lambda m: in_copy(e, m).start(), fine)
         weight_copy(e).start()
 
     @pl.when(e == 0)
@@ -376,8 +377,9 @@
 
     weight_copy(e).wait()
 
+    for_rows(meta[8, e] * UNIT, most, lambda m: in_copy(e, m).wait(), fine)
+
     def compute(m):
-        in_copy(e, m).wait()
         for c, size in column_tiles(cols, 256):
             got = jnp.dot(hin[slot, pl.ds(0, m), :], wbuf[slot, :, c : c + size], preferred_element_type=F32)
             ost[pl.ds(0, m), c : c + size] = got.astype(BF16)
@@ -450,7 +452,7 @@
     most, rows = 4 * slots_padded, n_experts * slots_padded
     half = tokens // 2
     shapes = ((tokens, F32), (half, F32), (half, BF16), (half, F32), (half, BF16), (half, BF16), (half, BF16))
-    deep = min(6, n_experts)
+    deep = min(5, n_experts)
     whole = lambda r: pl.BlockSpec((r, cols), lambda e: (0, 0))
     return pl.pallas_call(
         functools.partial(down_kernel, n_experts, start),
@@ -571,17 +573,15 @@
         hidden = (jax.nn.silu(g) * u).astype(BF16)
         shared = jnp.dot(hidden, s_down, preferred_element_type=F32)
 
-        meta, tab, shared = lax.optimization_barrier((meta, tab, shared))
         onehot, comb = build(meta, tab, tokens, slots_padded)
         zs = []
         for i, pieces in enumerate(((x,), (left_a, left_b), (right_a, right_b))):
             zs.append(dispatch(i, meta, onehot, pieces))
         h = gate_up(meta, onehot, zs, x_far, w_gate, w_up, slots_padded)
 
-        y = None
-        cols = width // CHUNKS
-        for c in range(CHUNKS):
-            start = c * cols
+        y, start = None, 0
+        for eighths in CHUNKS:
+            cols = width * eighths // 8
             own, left_sum, left_send, right_sum, right_send, far_a, far_b = down_combine(
                 meta, comb, h, w_down, slots_padded, start, cols
             )
@@ -591,6 +591,7 @@
             lefts[0] = right((right_sum + from_left.astype(F32)).astype(BF16))
             rights[1] = left((left_sum + from_right.astype(F32)).astype(BF16))
             y = final(own, shared, lefts, rights, y, start)
+            start += cols
         return y[None, None]
 
     token_spec = P("dp", "ep", None, None)

time: 405 us -> 404 us (level)
  Pallas kernels: 203 us -> 193 us
  waiting for transfers between devices: 79 us -> 83.8 us
    ppermute x16 -> x13, waiting for transfers between devices: 0.04 us -> 47.4 us  [solution(): left = lambda v: lax.ppermute(v, 'ep', to_left)]
    ppermute x16 -> x13, waiting for transfers between devices: 78.9 us -> 36.5 us  [solution(): right = lambda v: lax.ppermute(v, 'ep', to_right)]
    pallas_call x4 -> x3, Pallas kernels: 85.2 us -> 76.4 us  [down_combine(): pl.pallas_call(functools.partial(down_kernel, n_experts, start), grid=(n_...]
    ppermute x16 -> x13, starting transfers between devices: 50 us -> 47.7 us  [solution(): left = lambda v: lax.ppermute(v, 'ep', to_left)]
    pallas_call x4 -> x3, Pallas kernels: 13.9 us -> 12.3 us  [final(): pl.pallas_call(final_kernel, grid=(1,), out_shape=jax.ShapeDtypeStruct(sh...]
  transfers between devices with their start and end apart: 33 -> 27, of which waited for: 11 -> 8; matrix products, arithmetic and copies ran while one was open for 14% -> 14% of each run, Pallas kernels for 16% -> 15%
where the time goes in v2:
time: 404 us; the launch traced here: 397 us
  Pallas kernels  193 us (48%)
  waiting for transfers between devices  83.8 us (21%)
  starting transfers between devices  58.2 us (14%)
  matrix products  47.6 us (12%)
  local copies, waits for them, and re-layouts  7.64 us (2%)
  other arithmetic  5.51 us (1%)
    pallas_call x3, Pallas kernels, down_combine(): pl.pallas_call(functools.partial(down_kernel, n_experts, start), grid=(n_...  76.4 us
    pallas_call x1, Pallas kernels, gate_up(): pl.pallas_call(functools.partial(up_kernel, n_experts), grid=(n_experts,)...  72.8 us
    ppermute x13, starting transfers between devices, solution(): left = lambda v: lax.ppermute(v, 'ep', to_left)  47.7 us
    ppermute x13, waiting for transfers between devices, solution(): left = lambda v: lax.ppermute(v, 'ep', to_left)  47.4 us
    ppermute x13, waiting for transfers between devices, solution(): right = lambda v: lax.ppermute(v, 'ep', to_right)  36.5 us
    dot_general x1, matrix products, step(): shared = jnp.dot(hidden, s_down, preferred_element_type=F32)  31 us
    pallas_call x3, Pallas kernels, dispatch(): pl.pallas_call(functools.partial(dispatch_kernel, source, n_experts), out...  20.9 us
    dot_general x1, matrix products, step(): g = jnp.dot(x, s_gate, preferred_element_type=F32)  14.8 us
  transfers between devices with their start and end apart: 27, of which 8 were waited for; matrix products, arithmetic and copies ran while one was open for 14% of the time, Pallas kernels for 15%

profile of v2, /device:TPU:112, one launch (start us, length us, event | category | flops | bytes accessed | tf_op | source)
XLA Modules:
  0.0 396.6 jit_solution(3133008918104368632)
XLA Ops:
  0.0 0.7 convert_element_type.136
  0.8 0.8 fusion.18
  1.5 4.1 %collective-permute-start.2 = (bf16[6,3,768]{2,0,1:T(8,128)(2,1)S(1)}, bf16[6,3,768]{2,0,1:T(8,128)(2,1)S(1)}, u32[]{:S(2)}, u32[]{:S(2)}) collective-permute-start(bf16[6,3,768]{2,0,1:T(8,128)(2,1)S(1)} %get-tuple-element.63), channel_id=1, source_target_pairs={{0,2},{1,3},{2,0},{3,1},{4,6},{5,7},{6,4},{7,5},{8,10},{9,11},{10,... | collective-permute-start | bytes 82952 | tf_op jit(solution)/shard_map/ppermute | solution.py:562
  5.6 1.0 collective-permute-start.1
  6.6 1.0 collective-permute-start
  7.7 4.0 %slice_bitcast_fusion = (bf16[384,2048]{1,0:T(8,128)(2,1)}, bf16[384,2048]{1,0:T(8,128)(2,1)}) fusion(bf16[1,1,768,2048]{3,2,1,0:T(8,128)(2,1)} %param.10), kind=kLoop, calls=%fused_computation.9 | loop fusion | bytes 6291456 | tf_op jit(solution)/shard_map/slice | solution.py:563
  11.6 0.7 collective-permute-start.3
  12.4 2.5 collective-permute-start.5
  14.9 14.8 %fusion.35 = f32[768,2816]{1,0:T(8,128)} fusion(bf16[2048,2816]{1,0:T(8,128)(2,1)} %param.17, bf16[1,1,768,2048]{3,2,1,0:T(8,128)(2,1)S(1)} %copy-done), kind=kOutput, calls=%fused_computation.71 | convolution fusion | flops 8858370048 | bytes 23330816 | tf_op jit(solution)/shard_map/dot_general | solution.py:571
  29.7 0.1 collective-permute-start.4
  29.8 3.2 collective-permute-start.6
  33.2 0.1 copy.22
  33.4 0.2 compare_convert_fusion
  33.5 0.2 broadcast_multiply_fusion
  33.8 1.9 fusion.8
  35.6 0.1 select_reduce_fusion
  35.8 0.2 reduce_window_sum.23
  36.0 0.2 reduce_window_sum.22
  36.2 0.1 copy.23
  36.3 0.7 pad.4.tab
  37.1 0.6 pad_add_fusion.meta
  37.7 12.8 %collective-permute-done.3.refs_0_ = bf16[384,2048]{1,0:T(8,128)(2,1)} collective-permute-done((bf16[384,2048]{1,0:T(8,128)(2,1)}, bf16[384,2048]{1,0:T(8,128)(2,1)}, u32[]{:S(2)}, u32[]{:S(2)}) %collective-permute-start.3) | collective-permute-done | bytes 1572896 | tf_op jit(solution)/shard_map/ppermute | solution.py:511
  50.4 31.1 %collective-permute-done.6.refs_1_ = bf16[384,2048]{1,0:T(8,128)(2,1)} collective-permute-done((bf16[384,2048]{1,0:T(8,128)(2,1)}, bf16[384,2048]{1,0:T(8,128)(2,1)}, u32[]{:S(2)}, u32[]{:S(2)}) %collective-permute-start.6) | collective-permute-done | bytes 1572896 | tf_op jit(solution)/shard_map/ppermute | solution.py:512
  81.5 3.7 collective-permute-start.8
  85.2 10.7 %build.1 = (bf16[4,6,256,768]{3,2,1,0:T(8,128)(2,1)}, bf16[4,6,768,256]{3,2,1,0:T(8,128)(2,1)}) custom-call(s32[10,16]{1,0:T(8,128)} %pad_add_fusion.meta, f32[4,96,128]{2,1,0:T(8,128)} %pad.4.tab), custom_call_target="tpu_custom_call" | custom-call | flops 15000000512 | bytes 20000000 | tf_op jit(solution)/shard_map/build/pallas_call | solution.py:90
  95.8 6.8 %shard_map.100.z0 = bf16[1536,2048]{1,0:T(8,128)(2,1)} custom-call(s32[10,16]{1,0:T(8,128)} %pad_add_fusion.meta, bf16[4,6,256,768]{3,2,1,0:T(8,128)(2,1)} %get-tuple-element.29.onehot, bf16[768,2048]{1,0:T(8,128)(2,1)} %bitcast.43), custom_call_target="tpu_custom_call" | custom-call | flops 5000000000 | bytes 8000000 | tf_op jit(solution)/shard_map/pallas_call | solution.py:167
  102.6 6.8 %shard_map.101.z1 = bf16[1536,2048]{1,0:T(8,128)(2,1)} custom-call(s32[10,16]{1,0:T(8,128)} %pad_add_fusion.meta, bf16[4,6,256,768]{3,2,1,0:T(8,128)(2,1)} %get-tuple-element.29.onehot, bf16[384,2048]{1,0:T(8,128)(2,1)} %collective-permute-done.3.refs_0_, bf16[384,2048]{1,0:T(8,128)(2,1)} %collective-permute-done.4.refs_1_), custom_call_target="tpu_custom_call" | custom-call | flops 5000000000 | bytes 8000000 | tf_op jit(solution)/shard_map/pallas_call | solution.py:167
  109.5 7.3 %shard_map.102.z2 = bf16[1536,2048]{1,0:T(8,128)(2,1)} custom-call(s32[10,16]{1,0:T(8,128)} %pad_add_fusion.meta, bf16[4,6,256,768]{3,2,1,0:T(8,128)(2,1)} %get-tuple-element.29.onehot, bf16[384,2048]{1,0:T(8,128)(2,1)} %collective-permute-done.5.refs_0_, bf16[384,2048]{1,0:T(8,128)(2,1)} %collective-permute-done.6.refs_1_), custom_call_target="tpu_custom_call" | custom-call | flops 5000000000 | bytes 8000000 | tf_op jit(solution)/shard_map/pallas_call | solution.py:167
  116.8 0.5 collective-permute-done.8.x_b
  117.2 0.7 copy-done.2
  117.9 1.1 copy-done.3
  119.0 72.8 %gate_up.1.h = bf16[6144,1408]{1,0:T(8,128)(2,1)} custom-call(s32[10,16]{1,0:T(8,128)} %pad_add_fusion.meta, bf16[4,6,256,768]{3,2,1,0:T(8,128)(2,1)} %get-tuple-element.29.onehot, bf16[1536,2048]{1,0:T(8,128)(2,1)} %shard_map.100.z0, bf16[1536,2048]{1,0:T(8,128)(2,1)} %shard_map.101.z1, bf16[1536,2048]{1,0:T(8,128)(2,1)} %shard_map.102.z2, ...), custom_call_target="tpu_custom_call" | custom-call | flops 60000002048 | bytes 200000000 | tf_op jit(solution)/shard_map/gate_up/pallas_call | solution.py:307
  191.8 27.7 %shard_map.104 = (f32[768,768]{1,0:T(8,128)}, f32[384,768]{1,0:T(8,128)}, bf16[384,768]{1,0:T(8,128)(2,1)}, f32[384,768]{1,0:T(8,128)}, bf16[384,768]{1,0:T(8,12...) custom-call(s32[10,16]{1,0:T(8,128)} %pad_add_fusion.meta, bf16[4,6,768,256]{3,2,1,0:T(8,128)(2,1)} %get-tuple-element.28.comb, ...), custom_call_target="tpu_custom_call" | custom-call | flops 15000000512 | bytes 37500000 | tf_op jit(solution)/shard_map/pallas_call | solution.py:457
  219.5 27.7 %shard_map.105 = (f32[768,768]{1,0:T(8,128)}, f32[384,768]{1,0:T(8,128)}, bf16[384,768]{1,0:T(8,128)(2,1)}, f32[384,768]{1,0:T(8,128)}, bf16[384,768]{1,0:T(8,12...) custom-call(s32[10,16]{1,0:T(8,128)} %pad_add_fusion.meta, bf16[4,6,768,256]{3,2,1,0:T(8,128)(2,1)} %get-tuple-element.28.comb, ...), custom_call_target="tpu_custom_call" | custom-call | flops 15000000512 | bytes 37500000 | tf_op jit(solution)/shard_map/pallas_call | solution.py:457
  247.5 16.7 %collective-permute-start.25 = (bf16[384,768]{1,0:T(8,128)(2,1)}, bf16[384,768]{1,0:T(8,128)(2,1)S(1)}, u32[]{:S(2)}, u32[]{:S(2)}) collective-permute-start(bf16[384,768]{1,0:T(8,128)(2,1)} %get-tuple-element.50), channel_id=1, source_target_pairs={{0,3},{1,0},{2,1},{3,2},{4,7},{5,4},{6,5},{7,6},{8,11},{9,8},{10,9... | collective-permute-start | bytes 1769480 | tf_op jit(solution)/shard_map/ppermute | solution.py:512
  264.2 21.1 %shard_map.103 = (f32[768,512]{1,0:T(8,128)}, f32[384,512]{1,0:T(8,128)}, bf16[384,512]{1,0:T(8,128)(2,1)}, f32[384,512]{1,0:T(8,128)}, bf16[384,512]{1,0:T(8,12...) custom-call(s32[10,16]{1,0:T(8,128)} %pad_add_fusion.meta, bf16[4,6,768,256]{3,2,1,0:T(8,128)(2,1)} %get-tuple-element.28.comb, ...), custom_call_target="tpu_custom_call" | custom-call | flops 10000000000 | bytes 25000000 | tf_op jit(solution)/shard_map/pallas_call | solution.py:457
  285.3 1.8 collective-permute-start.17
  287.0 2.7 collective-permute-start.18
  289.8 1.9 collective-permute-start.19
  291.7 0.1 add_convert_fusion.3
  291.8 0.2 collective-permute-start.9
  292.0 3.1 collective-permute-start.13
  295.2 0.1 add_convert_fusion.1
  295.3 0.1 add_convert_fusion
  295.4 16.2 %collective-permute-done.9 = bf16[384,512]{1,0:T(8,128)(2,1)S(1)} collective-permute-done((bf16[384,512]{1,0:T(8,128)(2,1)}, bf16[384,512]{1,0:T(8,128)(2,1)S(1)}, u32[]{:S(2)}, u32[]{:S(2)}) %collective-permute-start.9) | collective-permute-done | bytes 393248 | tf_op jit(solution)/shard_map/ppermute | solution.py:511
  311.6 10.2 %collective-permute-done.13 = bf16[384,512]{1,0:T(8,128)(2,1)S(1)} collective-permute-done((bf16[384,512]{1,0:T(8,128)(2,1)}, bf16[384,512]{1,0:T(8,128)(2,1)S(1)}, u32[]{:S(2)}, u32[]{:S(2)}) %collective-permute-start.13) | collective-permute-done | bytes 393248 | tf_op jit(solution)/shard_map/ppermute | solution.py:512
  321.8 3.0 collective-permute-start.24
  324.9 1.8 collective-permute-start.22
  326.7 1.5 collective-permute-start.26
  328.2 0.9 add_convert_fusion.5
  329.1 0.1 add_convert_fusion.4
  329.2 0.9 add_convert_fusion.2
  330.2 0.8 copy-done.12
  331.0 0.5 collective-permute-start.11
  331.5 5.6 %collective-permute-done.24.r0 = bf16[384,768]{1,0:T(8,128)(2,1)} collective-permute-done((bf16[384,768]{1,0:T(8,128)(2,1)S(1)}, bf16[384,768]{1,0:T(8,128)(2,1)}, u32[]{:S(2)}, u32[]{:S(2)}) %collective-permute-start.24) | collective-permute-done | bytes 589856 | tf_op jit(solution)/shard_map/ppermute | solution.py:512
  337.1 3.8 collective-permute-start.12
  340.9 1.2 collective-permute-done.16.l0
  342.1 6.3 %collective-permute-done.22.l0 = bf16[384,768]{1,0:T(8,128)(2,1)} collective-permute-done((bf16[384,768]{1,0:T(8,128)(2,1)S(1)}, bf16[384,768]{1,0:T(8,128)(2,1)}, u32[]{:S(2)}, u32[]{:S(2)}) %collective-permute-start.22) | collective-permute-done | bytes 589856 | tf_op jit(solution)/shard_map/ppermute | solution.py:511
  348.4 1.7 collective-permute-start.14
  350.1 2.8 collective-permute-start.20
  352.9 31.0 %fusion.3.shared = f32[768,2048]{1,0:T(8,128)} fusion(bf16[2816,2048]{1,0:T(8,128)(2,1)} %param.19, f32[768,2816]{1,0:T(8,128)} %fusion.35, bf16[2048,2816]{1,0:T(8,128)(2,1)} %param.18, bf16[1,1,768,2048]{3,2,1,0:T(8,128)(2,1)S(1)} %copy-done.1), kind=kOutput, calls=%fused_computation.4 | convolution fusion | flops 17729716224 | bytes 41156608 | tf_op jit(solution)/shard_map/dot_general | solution.py:574
  383.9 4.4 %shard_map.106.refs_0_ = bf16[768,2048]{1,0:T(8,128)(2,1)} custom-call(f32[768,768]{1,0:T(8,128)} %get-tuple-element.44.own, f32[768,2048]{1,0:T(8,128)} %fusion.3.shared, bf16[384,768]{1,0:T(8,128)(2,1)} %collective-permute-done.22.l0, bf16[384,768]{1,0:T(8,128)(2,1)} %copy-done.12, bf16[384,768]{1,0:T(8,128)(2,1)} %collective-permute-done.24.r0, ...), custom_call_target="tpu_custom_call" | custom-call | flops 2000000000 | bytes 8000000 | tf_op jit(solution)/shard_map/pallas_call | solution.py:494
  388.3 4.4 %shard_map.107.refs_0_ = bf16[768,2048]{1,0:T(8,128)(2,1)} custom-call(f32[768,768]{1,0:T(8,128)} %get-tuple-element.37.own, f32[768,2048]{1,0:T(8,128)} %fusion.3.shared, bf16[384,768]{1,0:T(8,128)(2,1)} %collective-permute-done.16.l0, bf16[384,768]{1,0:T(8,128)(2,1)} %copy-done.10, bf16[384,768]{1,0:T(8,128)(2,1)} %copy-done.11, ...), custom_call_target="tpu_custom_call", output_to_operand_aliasing={{}: (6, {})} | custom-call | flops 2000000000 | bytes 8000000 | tf_op jit(solution)/shard_map/pallas_call | solution.py:494
  392.8 3.5 shard_map.108
  (74 shorter events, 0.6 us)
Async XLA Ops:
  1.5 13.4 %copy-start = (bf16[1,1,768,2048]{3,2,1,0:T(8,128)(2,1)S(1)}, bf16[1,1,768,2048]{3,2,1,0:T(8,128)(2,1)}, u32[]{:S(2)}) copy-start(bf16[1,1,768,2048]{3,2,1,0:T(8,128)(2,1)} %param.10) | copy-start | bytes 9437188
  1.5 28.2 %collective-permute-start.2 = (bf16[6,3,768]{2,0,1:T(8,128)(2,1)S(1)}, bf16[6,3,768]{2,0,1:T(8,128)(2,1)S(1)}, u32[]{:S(2)}, u32[]{:S(2)}) collective-permute-start(bf16[6,3,768]{2,0,1:T(8,128)(2,1)S(1)} %get-tuple-element.63), channel_id=1, source_target_pairs={{0,2},{1,3},{2,0},{3,1},{4,6},{5,7},{6,4},{7,5},{8,10},{9,11},{10,... | collective-permute-start | bytes 82952 | tf_op jit(solution)/shard_map/ppermute | solution.py:562
  5.6 24.2 %collective-permute-start.1 = (bf16[6,3,768]{2,0,1:T(8,128)(2,1)S(1)}, bf16[6,3,768]{2,0,1:T(8,128)(2,1)S(1)}, u32[]{:S(2)}, u32[]{:S(2)}) collective-permute-start(bf16[6,3,768]{2,0,1:T(8,128)(2,1)S(1)} %get-tuple-element.63), channel_id=1, source_target_pairs={{0,3},{1,0},{2,1},{3,2},{4,7},{5,4},{6,5},{7,6},{8,11},{9,8},{10,9... | collective-permute-start | bytes 82952 | tf_op jit(solution)/shard_map/ppermute | solution.py:512
  6.6 26.4 %collective-permute-start = (bf16[6,3,768]{2,0,1:T(8,128)(2,1)S(1)}, bf16[6,3,768]{2,0,1:T(8,128)(2,1)S(1)}, u32[]{:S(2)}, u32[]{:S(2)}) collective-permute-start(bf16[6,3,768]{2,0,1:T(8,128)(2,1)S(1)} %get-tuple-element.63), channel_id=1, source_target_pairs={{0,1},{1,2},{2,3},{3,0},{4,5},{5,6},{6,7},{7,4},{8,9},{9,10},{10,1... | collective-permute-start | bytes 82952 | tf_op jit(solution)/shard_map/ppermute | solution.py:511
  11.6 38.8 %collective-permute-start.3 = (bf16[384,2048]{1,0:T(8,128)(2,1)}, bf16[384,2048]{1,0:T(8,128)(2,1)}, u32[]{:S(2)}, u32[]{:S(2)}) collective-permute-start(bf16[384,2048]{1,0:T(8,128)(2,1)} %get-tuple-element.56), channel_id=1, source_target_pairs={{0,1},{1,2},{2,3},{3,0},{4,5},{5,6},{6,7},{7,4},{8,9},{9,10},{10,1... | collective-permute-start | bytes 4718600 | tf_op jit(solution)/shard_map/ppermute | solution.py:511
  12.4 97.1 %collective-permute-start.5 = (bf16[384,2048]{1,0:T(8,128)(2,1)}, bf16[384,2048]{1,0:T(8,128)(2,1)}, u32[]{:S(2)}, u32[]{:S(2)}) collective-permute-start(bf16[384,2048]{1,0:T(8,128)(2,1)} %get-tuple-element.56), channel_id=1, source_target_pairs={{0,3},{1,0},{2,1},{3,2},{4,7},{5,4},{6,5},{7,6},{8,11},{9,8},{10,9... | collective-permute-start | bytes 4718600 | tf_op jit(solution)/shard_map/ppermute | solution.py:512
  29.7 72.9 %collective-permute-start.4 = (bf16[384,2048]{1,0:T(8,128)(2,1)}, bf16[384,2048]{1,0:T(8,128)(2,1)}, u32[]{:S(2)}, u32[]{:S(2)}) collective-permute-start(bf16[384,2048]{1,0:T(8,128)(2,1)} %get-tuple-element.55), channel_id=1, source_target_pairs={{0,1},{1,2},{2,3},{3,0},{4,5},{5,6},{6,7},{7,4},{8,9},{9,10},{10,1... | collective-permute-start | bytes 4718600 | tf_op jit(solution)/shard_map/ppermute | solution.py:511
  29.8 51.7 %collective-permute-start.6 = (bf16[384,2048]{1,0:T(8,128)(2,1)}, bf16[384,2048]{1,0:T(8,128)(2,1)}, u32[]{:S(2)}, u32[]{:S(2)}) collective-permute-start(bf16[384,2048]{1,0:T(8,128)(2,1)} %get-tuple-element.55), channel_id=1, source_target_pairs={{0,3},{1,0},{2,1},{3,2},{4,7},{5,4},{6,5},{7,6},{8,11},{9,8},{10,9... | collective-permute-start | bytes 4718600 | tf_op jit(solution)/shard_map/ppermute | solution.py:512
  50.4 66.3 %collective-permute-start.7 = (bf16[384,2048]{1,0:T(8,128)(2,1)}, bf16[384,2048]{1,0:T(8,128)(2,1)S(1)}, u32[]{:S(2)}, u32[]{:S(2)}) collective-permute-start(bf16[384,2048]{1,0:T(8,128)(2,1)} %collective-permute-done.3.refs_0_), channel_id=1, source_target_pairs={{0,1},{1,2},{2,3},{3,0},{4,5},{5,6},{6,7},{7,4},{8,9},{9,10},{10,1... | collective-permute-start | bytes 4718600 | tf_op jit(solution)/shard_map/ppermute | solution.py:511
  81.5 35.8 %collective-permute-start.8 = (bf16[384,2048]{1,0:T(8,128)(2,1)}, bf16[384,2048]{1,0:T(8,128)(2,1)S(1)}, u32[]{:S(2)}, u32[]{:S(2)}) collective-permute-start(bf16[384,2048]{1,0:T(8,128)(2,1)} %collective-permute-done.6.refs_1_), channel_id=1, source_target_pairs={{0,3},{1,0},{2,1},{3,2},{4,7},{5,4},{6,5},{7,6},{8,11},{9,8},{10,9... | collective-permute-start | bytes 4718600 | tf_op jit(solution)/shard_map/ppermute | solution.py:512
  116.8 1.1 copy-start.2
  117.9 1.1 copy-start.3
  219.5 27.7 %copy-start.15 = (bf16[384,768]{1,0:T(8,128)(2,1)S(1)}, bf16[384,768]{1,0:T(8,128)(2,1)}, u32[]{:S(2)}) copy-start(bf16[384,768]{1,0:T(8,128)(2,1)} %get-tuple-element.39) | copy-start | bytes 1769476
  247.2 42.5 %collective-permute-start.15 = (bf16[384,768]{1,0:T(8,128)(2,1)S(1)}, bf16[384,768]{1,0:T(8,128)(2,1)S(1)}, u32[]{:S(2)}, u32[]{:S(2)}) collective-permute-start(bf16[384,768]{1,0:T(8,128)(2,1)S(1)} %copy-done.15), channel_id=1, source_target_pairs={{0,1},{1,2},{2,3},{3,0},{4,5},{5,6},{6,7},{7,4},{8,9},{9,10},{10,1... | collective-permute-start | bytes 1769480 | tf_op jit(solution)/shard_map/ppermute | solution.py:511
  247.3 44.5 %collective-permute-start.21 = (bf16[384,768]{1,0:T(8,128)(2,1)}, bf16[384,768]{1,0:T(8,128)(2,1)S(1)}, u32[]{:S(2)}, u32[]{:S(2)}) collective-permute-start(bf16[384,768]{1,0:T(8,128)(2,1)} %get-tuple-element.46), channel_id=1, source_target_pairs={{0,1},{1,2},{2,3},{3,0},{4,5},{5,6},{6,7},{7,4},{8,9},{9,10},{10,1... | collective-permute-start | bytes 1769480 | tf_op jit(solution)/shard_map/ppermute | solution.py:511
  247.4 44.2 %copy-start.7 = (f32[384,768]{1,0:T(8,128)S(1)}, f32[384,768]{1,0:T(8,128)}, u32[]{:S(2)}) copy-start(f32[384,768]{1,0:T(8,128)} %get-tuple-element.38) | copy-start | bytes 3538948
  247.5 44.6 %collective-permute-start.25 = (bf16[384,768]{1,0:T(8,128)(2,1)}, bf16[384,768]{1,0:T(8,128)(2,1)S(1)}, u32[]{:S(2)}, u32[]{:S(2)}) collective-permute-start(bf16[384,768]{1,0:T(8,128)(2,1)} %get-tuple-element.50), channel_id=1, source_target_pairs={{0,3},{1,0},{2,1},{3,2},{4,7},{5,4},{6,5},{7,6},{8,11},{9,8},{10,9... | collective-permute-start | bytes 1769480 | tf_op jit(solution)/shard_map/ppermute | solution.py:512
  285.2 9.9 %copy-start.6 = (f32[384,768]{1,0:T(8,128)S(1)}, f32[384,768]{1,0:T(8,128)}, u32[]{:S(2)}) copy-start(f32[384,768]{1,0:T(8,128)} %get-tuple-element.45) | copy-start | bytes 3538948
  285.2 10.0 %copy-start.5 = (f32[384,768]{1,0:T(8,128)S(1)}, f32[384,768]{1,0:T(8,128)}, u32[]{:S(2)}) copy-start(f32[384,768]{1,0:T(8,128)} %get-tuple-element.49) | copy-start | bytes 3538948
  285.3 39.6 %collective-permute-start.17 = (bf16[384,768]{1,0:T(8,128)(2,1)}, bf16[384,768]{1,0:T(8,128)(2,1)S(1)}, u32[]{:S(2)}, u32[]{:S(2)}) collective-permute-start(bf16[384,768]{1,0:T(8,128)(2,1)} %get-tuple-element.40), channel_id=1, source_target_pairs={{0,1},{1,2},{2,3},{3,0},{4,5},{5,6},{6,7},{7,4},{8,9},{9,10},{10,1... | collective-permute-start | bytes 1769480 | tf_op jit(solution)/shard_map/ppermute | solution.py:511
  287.0 37.8 %collective-permute-start.18 = (bf16[384,768]{1,0:T(8,128)(2,1)}, bf16[384,768]{1,0:T(8,128)(2,1)S(1)}, u32[]{:S(2)}, u32[]{:S(2)}) collective-permute-start(bf16[384,768]{1,0:T(8,128)(2,1)} %get-tuple-element.41), channel_id=1, source_target_pairs={{0,3},{1,0},{2,1},{3,2},{4,7},{5,4},{6,5},{7,6},{8,11},{9,8},{10,9... | collective-permute-start | bytes 1769480 | tf_op jit(solution)/shard_map/ppermute | solution.py:512
  289.8 36.9 %collective-permute-start.19 = (bf16[384,768]{1,0:T(8,128)(2,1)}, bf16[384,768]{1,0:T(8,128)(2,1)S(1)}, u32[]{:S(2)}, u32[]{:S(2)}) collective-permute-start(bf16[384,768]{1,0:T(8,128)(2,1)} %get-tuple-element.43), channel_id=1, source_target_pairs={{0,3},{1,0},{2,1},{3,2},{4,7},{5,4},{6,5},{7,6},{8,11},{9,8},{10,9... | collective-permute-start | bytes 1769480 | tf_op jit(solution)/shard_map/ppermute | solution.py:512
  291.7 19.9 %copy-start.14 = (bf16[384,768]{1,0:T(8,128)(2,1)S(1)}, bf16[384,768]{1,0:T(8,128)(2,1)}, u32[]{:S(2)}) copy-start(bf16[384,768]{1,0:T(8,128)(2,1)} %get-tuple-element.47) | copy-start | bytes 1769476
  291.7 30.1 %copy-start.13 = (bf16[384,768]{1,0:T(8,128)(2,1)S(1)}, bf16[384,768]{1,0:T(8,128)(2,1)}, u32[]{:S(2)}) copy-start(bf16[384,768]{1,0:T(8,128)(2,1)} %get-tuple-element.48) | copy-start | bytes 1769476
  291.7 36.5 %copy-start.9 = (f32[384,512]{1,0:T(8,128)S(1)}, f32[384,512]{1,0:T(8,128)}, u32[]{:S(2)}) copy-start(f32[384,512]{1,0:T(8,128)} %get-tuple-element.31) | copy-start | bytes 2359300
  291.8 19.8 %collective-permute-start.9 = (bf16[384,512]{1,0:T(8,128)(2,1)}, bf16[384,512]{1,0:T(8,128)(2,1)S(1)}, u32[]{:S(2)}, u32[]{:S(2)}) collective-permute-start(bf16[384,512]{1,0:T(8,128)(2,1)} %get-tuple-element.32), channel_id=1, source_target_pairs={{0,1},{1,2},{2,3},{3,0},{4,5},{5,6},{6,7},{7,4},{8,9},{9,10},{10,1... | collective-permute-start | bytes 1179656 | tf_op jit(solution)/shard_map/ppermute | solution.py:511
  292.0 29.8 %collective-permute-start.13 = (bf16[384,512]{1,0:T(8,128)(2,1)}, bf16[384,512]{1,0:T(8,128)(2,1)S(1)}, u32[]{:S(2)}, u32[]{:S(2)}) collective-permute-start(bf16[384,512]{1,0:T(8,128)(2,1)} %get-tuple-element.36), channel_id=1, source_target_pairs={{0,3},{1,0},{2,1},{3,2},{4,7},{5,4},{6,5},{7,6},{8,11},{9,8},{10,9... | collective-permute-start | bytes 1179656 | tf_op jit(solution)/shard_map/ppermute | solution.py:512
  295.2 33.9 %copy-start.8 = (f32[384,512]{1,0:T(8,128)S(1)}, f32[384,512]{1,0:T(8,128)}, u32[]{:S(2)}) copy-start(f32[384,512]{1,0:T(8,128)} %get-tuple-element.35) | copy-start | bytes 2359300
  295.3 33.9 %copy-start.4 = (f32[384,768]{1,0:T(8,128)S(1)}, f32[384,768]{1,0:T(8,128)}, u32[]{:S(2)}) copy-start(f32[384,768]{1,0:T(8,128)} %get-tuple-element.42) | copy-start | bytes 3538948
  295.4 57.5 %copy-start.1 = (bf16[1,1,768,2048]{3,2,1,0:T(8,128)(2,1)S(1)}, bf16[1,1,768,2048]{3,2,1,0:T(8,128)(2,1)}, u32[]{:S(2)}) copy-start(bf16[1,1,768,2048]{3,2,1,0:T(8,128)(2,1)} %param.10) | copy-start | bytes 9437188
  311.6 18.6 %collective-permute-start.23 = (bf16[384,768]{1,0:T(8,128)(2,1)S(1)}, bf16[384,768]{1,0:T(8,128)(2,1)S(1)}, u32[]{:S(2)}, u32[]{:S(2)}) collective-permute-start(bf16[384,768]{1,0:T(8,128)(2,1)S(1)} %copy-done.14), channel_id=1, source_target_pairs={{0,1},{1,2},{2,3},{3,0},{4,5},{5,6},{6,7},{7,4},{8,9},{9,10},{10,1... | collective-permute-start | bytes 1769480 | tf_op jit(solution)/shard_map/ppermute | solution.py:511
  321.8 15.3 %collective-permute-start.24 = (bf16[384,768]{1,0:T(8,128)(2,1)S(1)}, bf16[384,768]{1,0:T(8,128)(2,1)}, u32[]{:S(2)}, u32[]{:S(2)}) collective-permute-start(bf16[384,768]{1,0:T(8,128)(2,1)S(1)} %copy-done.13), channel_id=1, source_target_pairs={{0,3},{1,0},{2,1},{3,2},{4,7},{5,4},{6,5},{7,6},{8,11},{9,8},{10,9... | collective-permute-start | bytes 1769480 | tf_op jit(solution)/shard_map/ppermute | solution.py:512
  324.8 5.3 %copy-start.10 = (bf16[384,768]{1,0:T(8,128)(2,1)}, bf16[384,768]{1,0:T(8,128)(2,1)S(1)}, u32[]{:S(2)}) copy-start(bf16[384,768]{1,0:T(8,128)(2,1)S(1)} %collective-permute-done.17.l1) | copy-start | bytes 1769476
  324.8 17.2 %collective-permute-start.16 = (bf16[384,768]{1,0:T(8,128)(2,1)S(1)}, bf16[384,768]{1,0:T(8,128)(2,1)}, u32[]{:S(2)}, u32[]{:S(2)}) collective-permute-start(bf16[384,768]{1,0:T(8,128)(2,1)S(1)} %add_convert_fusion.3), channel_id=1, source_target_pairs={{0,1},{1,2},{2,3},{3,0},{4,5},{5,6},{6,7},{7,4},{8,9},{9,10},{10,1... | collective-permute-start | bytes 1769480 | tf_op jit(solution)/shard_map/ppermute | solution.py:511
  324.9 5.3 %copy-start.11 = (bf16[384,768]{1,0:T(8,128)(2,1)}, bf16[384,768]{1,0:T(8,128)(2,1)S(1)}, u32[]{:S(2)}) copy-start(bf16[384,768]{1,0:T(8,128)(2,1)S(1)} %collective-permute-done.18.r0) | copy-start | bytes 1769476
  324.9 23.5 %collective-permute-start.22 = (bf16[384,768]{1,0:T(8,128)(2,1)S(1)}, bf16[384,768]{1,0:T(8,128)(2,1)}, u32[]{:S(2)}, u32[]{:S(2)}) collective-permute-start(bf16[384,768]{1,0:T(8,128)(2,1)S(1)} %add_convert_fusion.1), channel_id=1, source_target_pairs={{0,1},{1,2},{2,3},{3,0},{4,5},{5,6},{6,7},{7,4},{8,9},{9,10},{10,1... | collective-permute-start | bytes 1769480 | tf_op jit(solution)/shard_map/ppermute | solution.py:511
  326.7 23.4 %collective-permute-start.26 = (bf16[384,768]{1,0:T(8,128)(2,1)S(1)}, bf16[384,768]{1,0:T(8,128)(2,1)}, u32[]{:S(2)}, u32[]{:S(2)}) collective-permute-start(bf16[384,768]{1,0:T(8,128)(2,1)S(1)} %add_convert_fusion), channel_id=1, source_target_pairs={{0,3},{1,0},{2,1},{3,2},{4,7},{5,4},{6,5},{7,6},{8,11},{9,8},{10,9... | collective-permute-start | bytes 1769480 | tf_op jit(solution)/shard_map/ppermute | solution.py:512
  330.2 0.8 copy-start.12
  331.0 61.8 %collective-permute-start.11 = (bf16[384,512]{1,0:T(8,128)(2,1)}, bf16[384,512]{1,0:T(8,128)(2,1)}, u32[]{:S(2)}, u32[]{:S(2)}) collective-permute-start(bf16[384,512]{1,0:T(8,128)(2,1)} %get-tuple-element.33), channel_id=1, source_target_pairs={{0,1},{1,2},{2,3},{3,0},{4,5},{5,6},{6,7},{7,4},{8,9},{9,10},{10,1... | collective-permute-start | bytes 1179656 | tf_op jit(solution)/shard_map/ppermute | solution.py:511
  337.1 55.6 %collective-permute-start.12 = (bf16[384,512]{1,0:T(8,128)(2,1)}, bf16[384,512]{1,0:T(8,128)(2,1)}, u32[]{:S(2)}, u32[]{:S(2)}) collective-permute-start(bf16[384,512]{1,0:T(8,128)(2,1)} %get-tuple-element.34), channel_id=1, source_target_pairs={{0,3},{1,0},{2,1},{3,2},{4,7},{5,4},{6,5},{7,6},{8,11},{9,8},{10,9... | collective-permute-start | bytes 1179656 | tf_op jit(solution)/shard_map/ppermute | solution.py:512
  342.1 50.7 %collective-permute-start.10 = (bf16[384,512]{1,0:T(8,128)(2,1)}, bf16[384,512]{1,0:T(8,128)(2,1)}, u32[]{:S(2)}, u32[]{:S(2)}) collective-permute-start(bf16[384,512]{1,0:T(8,128)(2,1)} %add_convert_fusion.5), channel_id=1, source_target_pairs={{0,1},{1,2},{2,3},{3,0},{4,5},{5,6},{6,7},{7,4},{8,9},{9,10},{10,1... | collective-permute-start | bytes 1179656 | tf_op jit(solution)/shard_map/ppermute | solution.py:511
  348.4 44.4 %collective-permute-start.14 = (bf16[384,512]{1,0:T(8,128)(2,1)S(1)}, bf16[384,512]{1,0:T(8,128)(2,1)}, u32[]{:S(2)}, u32[]{:S(2)}) collective-permute-start(bf16[384,512]{1,0:T(8,128)(2,1)S(1)} %add_convert_fusion.4), channel_id=1, source_target_pairs={{0,3},{1,0},{2,1},{3,2},{4,7},{5,4},{6,5},{7,6},{8,11},{9,8},{10,9... | collective-permute-start | bytes 1179656 | tf_op jit(solution)/shard_map/ppermute | solution.py:512
  350.1 38.2 %collective-permute-start.20 = (bf16[384,768]{1,0:T(8,128)(2,1)}, bf16[384,768]{1,0:T(8,128)(2,1)}, u32[]{:S(2)}, u32[]{:S(2)}) collective-permute-start(bf16[384,768]{1,0:T(8,128)(2,1)} %add_convert_fusion.2), channel_id=1, source_target_pairs={{0,3},{1,0},{2,1},{3,2},{4,7},{5,4},{6,5},{7,6},{8,11},{9,8},{10,9... | collective-permute-start | bytes 1769480 | tf_op jit(solution)/shard_map/ppermute | solution.py:512
